TPU v7x, 512 devices: a whole 4x4x16 slice. The times are simulated.
512 devices in a mesh: section: 16 (over y, x), seq: 8 (over z_lo, core), dp: 4 (over z_hi).
Axes of the slice: x: 4, y: 4, z: 16 (z_hi: 4, z_lo: 4; z = z_hi * 4 + z_lo), core: 2. Of those that a mesh axis runs over, the one named last changes fastest.
Arguments:
- stream: bfloat16 [16, 4, 1024, 1280], P('section', 'dp', 'seq'), may hold values from -16 to 16
- norm_gain: float32 [16, 1280], P('section'), may hold values from 0.25 to 1.75
- w_xbc: bfloat16 [16, 1280, 2688], P('section', ('seq', 'dp')), may hold values from -0.15625 to 0.15625
- w_dt: bfloat16 [16, 1280, 40], P('section', ('seq', 'dp')), may hold values from -0.15625 to 0.15625
- conv_weight: float32 [16, 4, 2688], P('section'), may hold values from -3 to 3
- conv_bias: float32 [16, 2688], P('section'), may hold values from -1.8 to 1.8
- dt_bias: float32 [16, 40], P('section'), may hold values from -1 to 1
- decay_rate: float32 [16, 40], P('section'), may hold values from 9.765625e-05 to 0.04
- skip_weight: float32 [16, 40], P('section'), may hold values from 0.5 to 1.5
- inner_gain: float32 [16, 2560], P('section'), may hold values from 0.25 to 1.75
- w_out: bfloat16 [16, 2560, 1280], P('section', ('seq', 'dp')), may hold values from -0.125 to 0.125
Outputs:
- next_stream: bfloat16 [16, 4, 1024, 1280], P('section', 'dp', 'seq')
All inputs are finite; a program needn't handle non-finite values.
Results may differ from a plain program's by a relative error of at most 0.008.
Values may be sent and summed in bfloat16 or wider, within the bound.
No kernel may reach another device: no remote copies, remote signals or barrier semaphores. Data moves between devices by JAX's collectives and lax.ppermute only.
A program may use at most 64 MiB of HBM per device.

v0:
```python
import jax
import jax.numpy as jnp
from jax import lax
from jax.experimental import pallas as pl
from jax.experimental.pallas import tpu as pltpu
from jax.sharding import Mesh
from jax.sharding import PartitionSpec as P

HEADS = 40
HEAD_DIM = 64
STATE = 64
CONV = 4
BLOCK = 128
INNER = 2560
D = 1280
SEQ = ("blk", "par", "core")
SEQ_DP = ("blk", "par", "core", "dp")
RING = ("blk", "core", "dp")
epsilon = 1e-05
LOCAL_HEADS = 10
LOCAL = LOCAL_HEADS * HEAD_DIM
TAPPED = LOCAL + 2 * STATE
WIDE = TAPPED + 128
ROWS = 512
PIECE = ROWS // BLOCK
HALF = D // 2


def ring_index(place, core):
    place = place % 8
    return (place % 2) * 8 + core * 4 + place // 2


def shifted(x, by):
    pairs = []
    for i in range(8):
        pairs.append((ring_index(i, 0), ring_index(i + by, 0)))
        pairs.append((ring_index(i, 1), ring_index(i - by, 1)))
    return lax.ppermute(x, RING, pairs)


def gathered(x, cut):
    up, down = x, x
    out = [x]
    for _ in range(1, 4):
        up, down = shifted(up, 1), shifted(down, -1)
        out += [up, down]
    half = x.shape[cut] // 2
    first = lax.slice_in_dim(up, 0, half, axis=cut)
    second = lax.slice_in_dim(down, half, 2 * half, axis=cut)
    out += [shifted(first, 1), shifted(second, -1)]
    return out


OFFSETS = (0, -1, 1, -2, 2, -3, 3, 4, 4)


def slot_of(place, offset):
    there = (place + offset + 8) % 8
    return (there % 2) * 4 + there // 2


def fill(where, chunks, scratch, cut):
    rows = chunks[0].shape[0]
    place, sign = where[0], where[1]
    for k in range(7):
        at = pl.multiple_of(slot_of(place, OFFSETS[k] * sign) * rows, 16)
        scratch[pl.ds(at, rows), :] = chunks[k][...]
    at = slot_of(place, 4) * rows
    if cut == 0:
        half = rows // 2
        scratch[pl.ds(pl.multiple_of(at, 16), half), :] = chunks[7][...]
        scratch[pl.ds(pl.multiple_of(at + half, 16), half), :] = chunks[8][...]
    else:
        half = chunks[7].shape[1]
        at = pl.multiple_of(at, 16)
        scratch[pl.ds(at, rows), :half] = chunks[7][...]
        scratch[pl.ds(at, rows), half:] = chunks[8][...]


def exact_dot(a, b):
    return jnp.dot(a, b, preferred_element_type=jnp.float32, precision=lax.Precision.HIGHEST)


def spread(per_head):
    rows = per_head.shape[0]
    left = lax.broadcasted_iota(jnp.int32, (rows, 128), 1) < HEAD_DIM
    pairs = []
    for p in range(LOCAL_HEADS // 2):
        first = jnp.broadcast_to(per_head[:, 2 * p : 2 * p + 1], (rows, 128))
        second = jnp.broadcast_to(per_head[:, 2 * p + 1 : 2 * p + 2], (rows, 128))
        pairs.append(jnp.where(left, first, second))
    return jnp.concatenate(pairs, axis=1)


def class_columns(x, group, width):
    found = None
    for g in range(4):
        piece = jnp.concatenate(
            [x[:, g * width : (g + 1) * width], x[:, (g + 4) * width : (g + 5) * width]], axis=1
        )
        found = piece if found is None else jnp.where(group == g, piece, found)
    return found


def class_heads(x, group, width, lanes):
    head = lax.broadcasted_iota(jnp.int32, (HEADS, lanes), 0)
    local = lax.broadcasted_iota(jnp.int32, (HEADS, lanes), 1) // width
    wanted = jnp.where(local < 5, group * 5 + local, 15 + group * 5 + local)
    select = jnp.logical_and(local < LOCAL_HEADS, head == wanted)
    return exact_dot(x, select.astype(jnp.float32))


def prep_kernel(where, all_taps, all_bias, all_dt_bias, all_rate, all_skip, all_gain, out):
    group = where[2]
    out[0:4, :LOCAL] = class_columns(all_taps[0], group, 320)
    out[0:4, LOCAL:] = all_taps[0, :, INNER:]
    out[4:5, :LOCAL] = class_columns(all_bias[...], group, 320)
    out[4:5, LOCAL:] = all_bias[:, INNER:]
    out[5:6, :LOCAL] = class_heads(all_skip[...], group, HEAD_DIM, LOCAL)
    out[6:7, :LOCAL] = class_columns(all_gain[...], group, 320)
    out[7:8, :128] = class_heads(all_dt_bias[...], group, 1, 128)
    out[8:9, :128] = class_heads(all_rate[...], group, 1, 128)


def mix_kernel(where, rows, halo, params, *rest):
    chunks, (y_out, c_out, grown_out, state_out, weight, raw) = rest[:9], rest[9:]
    fill(where, chunks, weight, 0)
    taps = params[0:4, :]
    bias = params[4:5, :]
    skip = params[5:6, :LOCAL]
    dt_bias = params[7:8, :128]
    rate = params[8:9, :128]
    projected = jnp.dot(rows[...], weight[...], preferred_element_type=jnp.float32)
    before = jnp.dot(halo[...], weight[:, :TAPPED], preferred_element_type=jnp.float32)
    raw[:8, :] = before.astype(jnp.bfloat16).astype(jnp.float32)
    raw[8:, :] = projected[:, :TAPPED].astype(jnp.bfloat16).astype(jnp.float32)
    shift = projected[:, TAPPED:] + dt_bias
    dt_all = jnp.maximum(shift, 0.0) + jnp.log1p(jnp.exp(-jnp.abs(shift)))
    row_id = lax.broadcasted_iota(jnp.int32, (BLOCK, BLOCK), 0)
    col_id = lax.broadcasted_iota(jnp.int32, (BLOCK, BLOCK), 1)
    causal = row_id >= col_id
    lower = causal.astype(jnp.float32)
    left = col_id < HEAD_DIM
    state = jnp.zeros((STATE, LOCAL), jnp.float32)
    decayed = jnp.ones((1, LOCAL), jnp.float32)
    for n in range(PIECE):
        at = n * BLOCK
        conv = bias + taps[0:1, :] * raw[at + 5 : at + 5 + BLOCK, :]
        for k in range(1, CONV):
            conv = conv + taps[k : k + 1, :] * raw[at + 5 + k : at + 5 + k + BLOCK, :]
        xbc = (conv / (1.0 + jnp.exp(-conv))).astype(jnp.bfloat16)
        values = xbc[:, :LOCAL]
        both = xbc[:, LOCAL:]
        b_rows, c_rows = both[:, :STATE], both[:, STATE:]
        dt = dt_all[at : at + BLOCK, :]
        cum = exact_dot(lower, -dt * rate)
        cum_t, dt_t = cum.T, dt.T
        scores = lax.dot_general(
            c_rows, b_rows, (((1,), (1,)), ((), ())), preferred_element_type=jnp.float32
        )
        scores = jnp.where(causal, scores, 0.0)
        intra = []
        for p in range(LOCAL_HEADS // 2):
            mixes = []
            for h in (2 * p, 2 * p + 1):
                lag = cum[:, h : h + 1] - cum_t[h : h + 1, :]
                weights = jnp.exp(jnp.minimum(lag, 0.0))
                mixes.append((scores * weights * dt_t[h : h + 1, :]).astype(jnp.bfloat16))
            pair = values[:, 128 * p : 128 * p + 128]
            none = jnp.zeros_like(pair)
            stacked = jnp.concatenate(
                [jnp.where(left, pair, none), jnp.where(left, none, pair)], axis=0
            )
            intra.append(
                jnp.dot(
                    jnp.concatenate(mixes, axis=1), stacked, preferred_element_type=jnp.float32
                )
            )
        wide = values.astype(jnp.float32)
        tail = spread(jnp.exp(cum[BLOCK - 1 :, :] - cum) * dt)
        growth = spread(jnp.exp(cum))
        scaled = (wide * tail).astype(jnp.bfloat16)
        local = jnp.concatenate(intra, axis=1) + skip * wide
        if n > 0:
            local = local + growth * exact_dot(c_rows.astype(jnp.float32), state)
        y_out[at : at + BLOCK, :] = local
        c_out[at : at + BLOCK, :] = c_rows
        grown_out[at : at + BLOCK, :] = growth * decayed
        summary = lax.dot_general(
            b_rows, scaled, (((0,), (0,)), ((), ())), preferred_element_type=jnp.float32
        )
        total = growth[BLOCK - 1 :, :]
        state = total * state + summary
        decayed = decayed * total
    state_out[...] = state.astype(jnp.bfloat16)


def pieces(square, lane):
    high = square.astype(jnp.bfloat16).astype(jnp.float32)
    middle = (square - high).astype(jnp.bfloat16).astype(jnp.float32)
    low = square - high - middle
    split = jnp.where(lane == 0, high, jnp.where(lane == 1, middle, jnp.where(lane == 2, low, 0.0)))
    return split.astype(jnp.bfloat16)


def out_kernel(where, y_in, c_in, grown, arriving, params, *rest):
    chunks, (keep_x, send_x, keep_y, send_y, weight, act, square, ordered) = rest[:9], rest[9:]
    fill(where, chunks, weight, 1)
    gain = params[6:7, :LOCAL]
    y = y_in[...] + grown[...] * jnp.dot(
        c_in[...], arriving[...], preferred_element_type=jnp.float32
    )
    act[...] = (y * gain).astype(jnp.bfloat16)
    square[...] = jnp.broadcast_to(jnp.sum(y * y, axis=1, keepdims=True), (ROWS, 128))
    par, core = where[3], where[4]
    starts = []
    for p in (par, 1 - par):
        for c in (core, 1 - core):
            starts.append(pl.multiple_of((p * 2 + c) * BLOCK, BLOCK))
    for k in range(4):
        ordered[k * BLOCK : (k + 1) * BLOCK, :] = act[pl.ds(starts[k], BLOCK), :]
    lane = lax.broadcasted_iota(jnp.int32, (BLOCK, 128), 1)
    result = jnp.dot(ordered[...], weight[...], preferred_element_type=jnp.float32)
    for k in range(4):
        part = result[k * BLOCK : (k + 1) * BLOCK, :]
        total = square[pl.ds(starts[k], BLOCK), :]
        if k % 2 == 0:
            keep_x[k // 2, :, :HALF] = part[:, :HALF]
            keep_x[k // 2, :, HALF:] = jnp.where(lane == 0, total, 0.0)
            keep_y[k // 2] = part[:, HALF:]
        else:
            send_x[k // 2, :, :HALF] = part[:, :HALF].astype(jnp.bfloat16)
            send_x[k // 2, :, HALF:] = pieces(total, lane)
            send_y[k // 2] = part[:, HALF:].astype(jnp.bfloat16)


def chip_kernel(keep, came, keep_out, send_out):
    keep_out[...] = keep[0] + came[0].astype(jnp.float32)
    leaving = keep[1] + came[1].astype(jnp.float32)
    send_out[:, :HALF] = leaving[:, :HALF].astype(jnp.bfloat16)
    if leaving.shape[1] > HALF:
        lane = lax.broadcasted_iota(jnp.int32, (BLOCK, 128), 1)
        total = jnp.sum(leaving[:, HALF:], axis=1, keepdims=True)
        send_out[:, HALF:] = pieces(jnp.broadcast_to(total, (BLOCK, 128)), lane)


def first_kernel(keep, came, rows, out, scale_out):
    total = keep[...] + came[...].astype(jnp.float32)
    square = jnp.sum(total[:, HALF:], axis=1, keepdims=True)
    scale = lax.rsqrt(square * (1.0 / INNER) + epsilon)
    scale_out[...] = jnp.broadcast_to(scale, (BLOCK, 128))
    wide = rows[:, :HALF].astype(jnp.float32)
    out[...] = (wide + total[:, :HALF] * scale).astype(jnp.bfloat16)


def second_kernel(keep, came, rows, scale, first, out):
    total = keep[...] + came[...].astype(jnp.float32)
    wide = rows[:, HALF:].astype(jnp.float32)
    out[0, 0, :, :HALF] = first[...]
    out[0, 0, :, HALF:] = (wide + total * scale[:, :1]).astype(jnp.bfloat16)


VMEM = pl.BlockSpec(memory_space=pltpu.VMEM)
SMEM = pl.BlockSpec(memory_space=pltpu.SMEM)


def called(kernel, outs, scratch, scalars, *arrays):
    return pl.pallas_call(
        kernel,
        out_shape=outs,
        in_specs=[SMEM] * len(scalars) + [VMEM] * len(arrays),
        out_specs=jax.tree.map(lambda _: VMEM, outs),
        scratch_shapes=scratch,
        compiler_params=pltpu.CompilerParams(vmem_limit_bytes=40 * 1024 * 1024),
    )(*scalars, *arrays)


def swapped(x, axis):
    return lax.ppermute(x, axis, [(0, 1), (1, 0)])


def onward(x):
    return lax.ppermute(x, "section", [(i, (i + 1) % 16) for i in range(16)])


def both_of(mine, theirs, index):
    first = jnp.where(index == 0, mine, theirs)
    second = jnp.where(index == 0, theirs, mine)
    return jnp.stack([first, second])


def shards(
    stream,
    norm_gain,
    w_xbc,
    w_dt,
    conv_weight,
    conv_bias,
    dt_bias,
    decay_rate,
    skip_weight,
    inner_gain,
    w_out,
):
    par, core = lax.axis_index("par"), lax.axis_index("core")
    group = par * 2 + core
    place = lax.axis_index("dp") * 2 + lax.axis_index("blk")
    where = jnp.stack([place, 1 - 2 * core, group, par, core]).astype(jnp.int32)

    out_chunks = gathered(onward(w_out[0]), 1)
    raw = onward(jnp.concatenate([w_xbc[0], w_dt[0]], axis=1))
    xbc, dtw = raw[:, : INNER + 2 * STATE], raw[:, INNER + 2 * STATE :]
    inner = xbc[:, :INNER].reshape(40, 2, 4, 320).transpose(2, 0, 1, 3).reshape(4, 40, LOCAL)
    shared = jnp.broadcast_to(xbc[None, :, INNER:], (4, 40, 2 * STATE))
    steps = dtw.reshape(40, 2, 4, 5).transpose(2, 0, 1, 3).reshape(4, 40, LOCAL_HEADS)
    steps = jnp.pad(steps, ((0, 0), (0, 0), (0, 128 - LOCAL_HEADS)))
    packed = jnp.concatenate([inner, shared, steps], axis=2)
    classes = lax.all_to_all(packed, ("par", "core"), 0, 0).reshape(160, WIDE)
    in_chunks = gathered(classes, 0)

    rows_in = stream[0, 0]
    wide = rows_in.astype(jnp.float32)
    mean_square = jnp.mean(wide * wide, axis=-1, keepdims=True)
    normed = (wide * lax.rsqrt(mean_square + epsilon) * norm_gain[0]).astype(jnp.bfloat16)
    feature = lax.broadcasted_iota(jnp.int32, (D, D), 0)
    target = lax.broadcasted_iota(jnp.int32, (D, D), 1)
    source = (target // 640) * 640 + (target // 40 % 4) * 160 + (target // 160 % 4) * 40 + target % 40
    select = (feature == source).astype(jnp.bfloat16)
    normed = jnp.dot(normed, select, preferred_element_type=jnp.float32).astype(jnp.bfloat16)
    normed = onward(normed)
    pair = both_of(normed, swapped(normed, "par"), par)
    quad = both_of(pair, swapped(pair, "core"), core)
    rows = quad.transpose(1, 0, 2, 3).reshape(ROWS, D)
    halo = lax.ppermute(rows[ROWS - 8 :], "blk", [(0, 1)])

    f32, bf16 = jnp.float32, jnp.bfloat16
    params = called(
        prep_kernel,
        jax.ShapeDtypeStruct((16, TAPPED), f32),
        [],
        (where,),
        conv_weight,
        conv_bias,
        dt_bias,
        decay_rate,
        skip_weight,
        inner_gain,
    )
    params = onward(params)
    residual = onward(rows_in)
    y_local, c_rows, grown, state = called(
        mix_kernel,
        (
            jax.ShapeDtypeStruct((ROWS, LOCAL), f32),
            jax.ShapeDtypeStruct((ROWS, STATE), bf16),
            jax.ShapeDtypeStruct((ROWS, LOCAL), f32),
            jax.ShapeDtypeStruct((STATE, LOCAL), bf16),
        ),
        [pltpu.VMEM((D, WIDE), bf16), pltpu.VMEM((ROWS + 8, TAPPED), f32)],
        (where,),
        rows,
        halo,
        params,
        *in_chunks,
    )
    arriving = lax.ppermute(state, "blk", [(0, 1)])

    shape = jax.ShapeDtypeStruct
    wide = HALF + 128
    keep_x, send_x, keep_y, send_y = called(
        out_kernel,
        (
            shape((2, BLOCK, wide), f32),
            shape((2, BLOCK, wide), bf16),
            shape((2, BLOCK, HALF), f32),
            shape((2, BLOCK, HALF), bf16),
        ),
        [
            pltpu.VMEM((LOCAL, D), bf16),
            pltpu.VMEM((ROWS, LOCAL), bf16),
            pltpu.VMEM((ROWS, 128), f32),
            pltpu.VMEM((ROWS, LOCAL), bf16),
        ],
        (where,),
        y_local,
        c_rows,
        grown,
        arriving,
        params,
        *out_chunks,
    )
    came_x, came_y = swapped(send_x, "core"), swapped(send_y, "core")
    keep_x, send_x = called(
        chip_kernel, (shape((BLOCK, wide), f32), shape((BLOCK, wide), bf16)), [], (), keep_x, came_x
    )
    came_x = swapped(send_x, "par")
    keep_y, send_y = called(
        chip_kernel, (shape((BLOCK, HALF), f32), shape((BLOCK, HALF), bf16)), [], (), keep_y, came_y
    )
    came_y = swapped(send_y, "par")
    next_x, scale = called(
        first_kernel,
        (shape((BLOCK, HALF), bf16), shape((BLOCK, 128), f32)),
        [],
        (),
        keep_x,
        came_x,
        residual,
    )
    return called(
        second_kernel,
        shape((1, 1, BLOCK, D), bf16),
        [],
        (),
        keep_y,
        came_y,
        residual,
        scale,
        next_x,
    )


def solution(mesh):
    torus = Mesh(
        mesh.devices.reshape(mesh.shape["section"], 2, 2, 2, mesh.shape["dp"]),
        ("section", "blk", "par", "core", "dp"),
    )
    return jax.shard_map(
        shards,
        mesh=torus,
        in_specs=(
            P("section", "dp", SEQ, None),
            P("section", None),
            P("section", SEQ_DP, None),
            P("section", SEQ_DP, None),
            P("section", None, None),
            P("section", None),
            P("section", None),
            P("section", None),
            P("section", None),
            P("section", None),
            P("section", SEQ_DP, None),
        ),
        out_specs=P("section", "dp", SEQ, None),
        check_vma=False,
    )
```

profile of v0, /device:TPU:1, one launch (start us, length us, event | category | flops | bytes accessed | tf_op | source)
XLA Modules:
  0.0 180.2 jit_solution(272474067930408843)
XLA Ops:
  1.9 2.6 %fusion.28 = bf16[128,1280]{1,0:T(8,128)(2,1)S(1)} fusion(s32[1280]{0:T(1024)S(1)} %get-tuple-element.39, s32[1280]{0:T(1024)S(1)} %get-tuple-element.41, s32[1280]{0:T(1024)S(1)} %get-tuple-element.37, s32[1280]{0:T(1024)S(1)} %get-tuple-element.42, s32[1280]{0:T(1024)S(1)} %get-tuple-element.38, s32[1280]{0:T(1024)S(1)} %get-tuple-element.47, ...), kind=kOutput, calls=%fused_computation.37 | convolution fusion | flops 474316800 | bytes 707072 | tf_op jit(solution)/shard_map/dot_general | solution.py:330
  4.6 3.9 %collective-permute-start = (bf16[128,1280]{1,0:T(8,128)(2,1)S(1)}, bf16[128,1280]{1,0:T(8,128)(2,1)S(1)}, u32[]{:S(2)}, u32[]{:S(2)}) collective-permute-start(bf16[128,1280]{1,0:T(8,128)(2,1)S(1)} %fusion.28), channel_id=1, source_target_pairs={{0,32},{32,64},{64,96},{96,128},{128,160},{160,192},{192,224},{224... | collective-permute-start | bytes 983048 | tf_op jit(solution)/shard_map/ppermute | solution.py:284
  8.5 3.1 %collective-permute-start.5 = (bf16[40,2728]{1,0:T(8,128)(2,1)S(1)}, bf16[40,2728]{1,0:T(8,128)(2,1)S(1)}, u32[]{:S(2)}, u32[]{:S(2)}) collective-permute-start(bf16[40,2728]{1,0:T(8,128)(2,1)S(1)} %pad_maximum_fusion.1), channel_id=1, source_target_pairs={{0,32},{32,64},{64,96},{96,128},{128,160},{160,192},{192,224},{224... | collective-permute-start | bytes 654728 | tf_op jit(solution)/shard_map/ppermute | solution.py:284
  11.7 5.0 %collective-permute-done = bf16[128,1280]{1,0:T(8,128)(2,1)S(1)} collective-permute-done((bf16[128,1280]{1,0:T(8,128)(2,1)S(1)}, bf16[128,1280]{1,0:T(8,128)(2,1)S(1)}, u32[]{:S(2)}, u32[]{:S(2)}) %collective-permute-start) | collective-permute-done | bytes 327712 | tf_op jit(solution)/shard_map/ppermute | solution.py:284
  16.7 6.4 %collective-permute-start.1 = (bf16[128,1280]{1,0:T(8,128)(2,1)S(1)}, bf16[128,1280]{1,0:T(8,128)(2,1)S(1)}, u32[]{:S(2)}, u32[]{:S(2)}) collective-permute-start(bf16[128,1280]{1,0:T(8,128)(2,1)S(1)} %collective-permute-done), channel_id=1, source_target_pairs={{0,8},{8,0},{1,9},{9,1},{2,10},{10,2},{3,11},{11,3},{4,12},{12,4},... | collective-permute-start | bytes 983048 | tf_op jit(solution)/shard_map/ppermute | solution.py:280
  24.8 6.5 %all-to-all-start = ((bf16[4,40,896]{2,1,0:T(8,128)(2,1)}), bf16[4,40,896]{2,1,0:T(8,128)(2,1)S(1)}, u32[]{:S(2)}, u32[]{:S(2)}) async-start(bf16[4,40,896]{2,1,0:T(8,128)(2,1)} %fusion.38), calls=%async_computation | async-start | bytes 573440 | tf_op jit(solution)/shard_map/all_to_all | solution.py:319
  34.2 2.0 %collective-permute-start.2 = (bf16[2,128,1280]{2,1,0:T(8,128)(2,1)}, bf16[2,128,1280]{2,1,0:T(8,128)(2,1)}, u32[]{:S(2)}, u32[]{:S(2)}) collective-permute-start(bf16[2,128,1280]{2,1,0:T(8,128)(2,1)} %pad_maximum_fusion), channel_id=1, source_target_pairs={{0,4},{4,0},{1,5},{5,1},{2,6},{6,2},{3,7},{7,3},{8,12},{12,8},{9,1... | collective-permute-start | bytes 1966088 | tf_op jit(solution)/shard_map/ppermute | solution.py:280
  36.2 6.8 %collective-permute-done.15.rest_0_ = bf16[80,1280]{1,0:T(8,128)(2,1)S(1)} collective-permute-done((bf16[80,1280]{1,0:T(8,128)(2,1)S(1)}, bf16[80,1280]{1,0:T(8,128)(2,1)S(1)}, u32[]{:S(2)}, u32[]{:S(2)}) %collective-permute-start.15) | collective-permute-done | bytes 204832 | tf_op jit(solution)/shard_map/ppermute | solution.py:284
  43.0 11.2 %collective-permute-start.16 = (bf16[80,1280]{1,0:T(8,128)(2,1)S(1)}, bf16[80,1280]{1,0:T(8,128)(2,1)S(1)}, u32[]{:S(2)}, u32[]{:S(2)}) collective-permute-start(bf16[80,1280]{1,0:T(8,128)(2,1)S(1)} %collective-permute-done.15.rest_0_), channel_id=1, source_target_pairs={{0,16},{4,23},{16,1},{20,4},{1,17},{5,20},{17,2},{21,5},{2,18},{6,... | collective-permute-start | bytes 614408 | tf_op jit(solution)/shard_map/ppermute | solution.py:39
  54.2 3.1 %collective-permute-start.6 = (bf16[160,896]{1,0:T(8,128)(2,1)S(1)}, bf16[160,896]{1,0:T(8,128)(2,1)S(1)}, u32[]{:S(2)}, u32[]{:S(2)}) collective-permute-start(bf16[160,896]{1,0:T(8,128)(2,1)S(1)} %bitcast.33), channel_id=1, source_target_pairs={{0,16},{4,23},{16,1},{20,4},{1,17},{5,20},{17,2},{21,5},{2,18},{6,... | collective-permute-start | bytes 860168 | tf_op jit(solution)/shard_map/ppermute | solution.py:39
  57.3 3.1 %collective-permute-start.7 = (bf16[160,896]{1,0:T(8,128)(2,1)S(1)}, bf16[160,896]{1,0:T(8,128)(2,1)S(1)}, u32[]{:S(2)}, u32[]{:S(2)}) collective-permute-start(bf16[160,896]{1,0:T(8,128)(2,1)S(1)} %bitcast.34), channel_id=1, source_target_pairs={{0,19},{4,20},{16,0},{20,5},{1,16},{5,21},{17,1},{21,6},{2,17},{6,... | collective-permute-start | bytes 860168 | tf_op jit(solution)/shard_map/ppermute | solution.py:39
  60.4 1.9 %collective-permute-start.17 = (bf16[80,1280]{1,0:T(8,128)(2,1)S(1)}, bf16[80,1280]{1,0:T(8,128)(2,1)S(1)}, u32[]{:S(2)}, u32[]{:S(2)}) collective-permute-start(bf16[80,1280]{1,0:T(8,128)(2,1)S(1)} %collective-permute-done.15.rest_0_), channel_id=1, source_target_pairs={{0,19},{4,20},{16,0},{20,5},{1,16},{5,21},{17,1},{21,6},{2,17},{6,... | collective-permute-start | bytes 614408 | tf_op jit(solution)/shard_map/ppermute | solution.py:39
  62.3 5.5 %collective-permute-start.18 = (bf16[80,1280]{1,0:T(8,128)(2,1)S(1)}, bf16[80,1280]{1,0:T(8,128)(2,1)S(1)}, u32[]{:S(2)}, u32[]{:S(2)}) collective-permute-start(bf16[80,1280]{1,0:T(8,128)(2,1)S(1)} %collective-permute-done.16.rest_1_), channel_id=1, source_target_pairs={{0,16},{4,23},{16,1},{20,4},{1,17},{5,20},{17,2},{21,5},{2,18},{6,... | collective-permute-start | bytes 614408 | tf_op jit(solution)/shard_map/ppermute | solution.py:39
  68.3 6.3 %collective-permute-start.8 = (bf16[160,896]{1,0:T(8,128)(2,1)S(1)}, bf16[160,896]{1,0:T(8,128)(2,1)S(1)}, u32[]{:S(2)}, u32[]{:S(2)}) collective-permute-start(bf16[160,896]{1,0:T(8,128)(2,1)S(1)} %collective-permute-done.6.rest_1_), channel_id=1, source_target_pairs={{0,16},{4,23},{16,1},{20,4},{1,17},{5,20},{17,2},{21,5},{2,18},{6,... | collective-permute-start | bytes 860168 | tf_op jit(solution)/shard_map/ppermute | solution.py:39
  74.6 3.9 %collective-permute-start.9 = (bf16[160,896]{1,0:T(8,128)(2,1)S(1)}, bf16[160,896]{1,0:T(8,128)(2,1)S(1)}, u32[]{:S(2)}, u32[]{:S(2)}) collective-permute-start(bf16[160,896]{1,0:T(8,128)(2,1)S(1)} %collective-permute-done.7.rest_2_), channel_id=1, source_target_pairs={{0,19},{4,20},{16,0},{20,5},{1,16},{5,21},{17,1},{21,6},{2,17},{6,... | collective-permute-start | bytes 860168 | tf_op jit(solution)/shard_map/ppermute | solution.py:39
  78.6 6.4 %collective-permute-start.19 = (bf16[80,1280]{1,0:T(8,128)(2,1)S(1)}, bf16[80,1280]{1,0:T(8,128)(2,1)S(1)}, u32[]{:S(2)}, u32[]{:S(2)}) collective-permute-start(bf16[80,1280]{1,0:T(8,128)(2,1)S(1)} %collective-permute-done.17.rest_2_), channel_id=1, source_target_pairs={{0,19},{4,20},{16,0},{20,5},{1,16},{5,21},{17,1},{21,6},{2,17},{6,... | collective-permute-start | bytes 614408 | tf_op jit(solution)/shard_map/ppermute | solution.py:39
  87.8 9.0 %collective-permute-done.19.rest_4_ = bf16[80,1280]{1,0:T(8,128)(2,1)S(1)} collective-permute-done((bf16[80,1280]{1,0:T(8,128)(2,1)S(1)}, bf16[80,1280]{1,0:T(8,128)(2,1)S(1)}, u32[]{:S(2)}, u32[]{:S(2)}) %collective-permute-start.19) | collective-permute-done | bytes 204832 | tf_op jit(solution)/shard_map/ppermute | solution.py:39
  98.8 2.7 %collective-permute-start.21 = (bf16[80,1280]{1,0:T(8,128)(2,1)S(1)}, bf16[80,1280]{1,0:T(8,128)(2,1)S(1)}, u32[]{:S(2)}, u32[]{:S(2)}) collective-permute-start(bf16[80,1280]{1,0:T(8,128)(2,1)S(1)} %collective-permute-done.19.rest_4_), channel_id=1, source_target_pairs={{0,19},{4,20},{16,0},{20,5},{1,16},{5,21},{17,1},{21,6},{2,17},{6,... | collective-permute-start | bytes 614408 | tf_op jit(solution)/shard_map/ppermute | solution.py:39
  101.5 4.7 %collective-permute-start.10 = (bf16[160,896]{1,0:T(8,128)(2,1)S(1)}, bf16[160,896]{1,0:T(8,128)(2,1)S(1)}, u32[]{:S(2)}, u32[]{:S(2)}) collective-permute-start(bf16[160,896]{1,0:T(8,128)(2,1)S(1)} %collective-permute-done.8.rest_3_), channel_id=1, source_target_pairs={{0,16},{4,23},{16,1},{20,4},{1,17},{5,20},{17,2},{21,5},{2,18},{6,... | collective-permute-start | bytes 860168 | tf_op jit(solution)/shard_map/ppermute | solution.py:39
  106.2 6.5 %collective-permute-start.11 = (bf16[160,896]{1,0:T(8,128)(2,1)S(1)}, bf16[160,896]{1,0:T(8,128)(2,1)S(1)}, u32[]{:S(2)}, u32[]{:S(2)}) collective-permute-start(bf16[160,896]{1,0:T(8,128)(2,1)S(1)} %collective-permute-done.9.rest_4_), channel_id=1, source_target_pairs={{0,19},{4,20},{16,0},{20,5},{1,16},{5,21},{17,1},{21,6},{2,17},{6,... | collective-permute-start | bytes 860168 | tf_op jit(solution)/shard_map/ppermute | solution.py:39
  114.0 4.2 %collective-permute-done.10.rest_5_ = bf16[160,896]{1,0:T(8,128)(2,1)S(1)} collective-permute-done((bf16[160,896]{1,0:T(8,128)(2,1)S(1)}, bf16[160,896]{1,0:T(8,128)(2,1)S(1)}, u32[]{:S(2)}, u32[]{:S(2)}) %collective-permute-start.10) | collective-permute-done | bytes 286752 | tf_op jit(solution)/shard_map/ppermute | solution.py:39
  118.2 9.4 %collective-permute-start.12 = (bf16[80,896]{1,0:T(8,128)(2,1)S(1)}, bf16[80,896]{1,0:T(8,128)(2,1)S(1)}, u32[]{:S(2)}, u32[]{:S(2)}) collective-permute-start(bf16[80,896]{1,0:T(8,128)(2,1)S(1)} %slice.39), channel_id=1, source_target_pairs={{0,16},{4,23},{16,1},{20,4},{1,17},{5,20},{17,2},{21,5},{2,18},{6,... | collective-permute-start | bytes 430088 | tf_op jit(solution)/shard_map/ppermute | solution.py:39
  127.7 2.1 %collective-permute-done.11.rest_6_ = bf16[160,896]{1,0:T(8,128)(2,1)S(1)} collective-permute-done((bf16[160,896]{1,0:T(8,128)(2,1)S(1)}, bf16[160,896]{1,0:T(8,128)(2,1)S(1)}, u32[]{:S(2)}, u32[]{:S(2)}) %collective-permute-start.11) | collective-permute-done | bytes 286752 | tf_op jit(solution)/shard_map/ppermute | solution.py:39
  132.0 2.7 %collective-permute-start.3 = (bf16[8,1280]{1,0:T(8,128)(2,1)S(1)}, bf16[8,1280]{1,0:T(8,128)(2,1)S(1)}, u32[]{:S(2)}, u32[]{:S(2)}) collective-permute-start(bf16[8,1280]{1,0:T(8,128)(2,1)S(1)} %slice.35), channel_id=1, source_target_pairs={{0,16},{1,17},{2,18},{3,19},{4,20},{5,21},{6,22},{7,23},{8,24},{9,... | collective-permute-start | bytes 61448 | tf_op jit(solution)/shard_map/ppermute | solution.py:335
  134.7 4.1 %collective-permute-start.22 = (bf16[80,640]{1,0:T(8,128)(2,1)S(1)}, bf16[80,640]{1,0:T(8,128)(2,1)S(1)}, u32[]{:S(2)}, u32[]{:S(2)}) collective-permute-start(bf16[80,640]{1,0:T(8,128)(2,1)S(1)} %slice.41), channel_id=1, source_target_pairs={{0,16},{4,23},{16,1},{20,4},{1,17},{5,20},{17,2},{21,5},{2,18},{6,... | collective-permute-start | bytes 307208 | tf_op jit(solution)/shard_map/ppermute | solution.py:39
  138.8 2.1 %collective-permute-start.23 = (bf16[80,640]{1,0:T(8,128)(2,1)S(1)}, bf16[80,640]{1,0:T(8,128)(2,1)S(1)}, u32[]{:S(2)}, u32[]{:S(2)}) collective-permute-start(bf16[80,640]{1,0:T(8,128)(2,1)S(1)} %slice.42), channel_id=1, source_target_pairs={{0,19},{4,20},{16,0},{20,5},{1,16},{5,21},{17,1},{21,6},{2,17},{6,... | collective-permute-start | bytes 307208 | tf_op jit(solution)/shard_map/ppermute | solution.py:39
  141.6 7.6 %shard_map.110 = (f32[512,640]{1,0:T(8,128)S(1)}, bf16[512,64]{1,0:T(8,128)(2,1)S(1)}, f32[512,640]{1,0:T(8,128)S(1)}, bf16[64,640]{1,0:T(8,128)(2,1)S(1)}) custom-call(s32[5]{0:T(128)S(1)} %stack.41.where, bf16[512,1280]{1,0:T(8,128)(2,1)S(1)} %bitcast.32, bf16[8,1280]{1,0:T(8,128)(2,1)S(1)} %collective-permute-done.3.halo, ...), custom_call_target="tpu_custom_call" | custom-call | tf_op jit(solution)/shard_map/pallas_call | solution.py:269
  149.2 5.5 %collective-permute-start.14 = (bf16[64,640]{1,0:T(8,128)(2,1)S(1)}, bf16[64,640]{1,0:T(8,128)(2,1)S(1)}, u32[]{:S(2)}, u32[]{:S(2)}) collective-permute-start(bf16[64,640]{1,0:T(8,128)(2,1)S(1)} %get-tuple-element.22), channel_id=1, source_target_pairs={{0,16},{1,17},{2,18},{3,19},{4,20},{5,21},{6,22},{7,23},{8,24},{9,... | collective-permute-start | bytes 245768 | tf_op jit(solution)/shard_map/ppermute | solution.py:367
  156.2 2.4 %shard_map.111 = (f32[2,128,768]{2,1,0:T(8,128)S(1)}, bf16[2,128,768]{2,1,0:T(8,128)(2,1)S(1)}, f32[2,128,640]{2,1,0:T(8,128)S(1)}, bf16[2,128,640]{2,1,0:T(8,128)(2,1)S(1)}) custom-call(s32[5]{0:T(128)S(1)} %stack.41.where, f32[512,640]{1,0:T(8,128)S(1)} %get-tuple-element.19.y_in, bf16[512,64]{1,0:T(8,128)(2,1)S(1)} %get-tuple-element.20.c_in, ...), custom_call_target="tpu_custom_call" | custom-call | tf_op jit(solution)/shard_map/pallas_call | solution.py:269
  158.6 4.6 %collective-permute-start.27 = (bf16[2,128,768]{2,1,0:T(8,128)(2,1)S(1)}, bf16[2,128,768]{2,1,0:T(8,128)(2,1)S(1)}, u32[]{:S(2)}, u32[]{:S(2)}) collective-permute-start(bf16[2,128,768]{2,1,0:T(8,128)(2,1)S(1)} %get-tuple-element.28), channel_id=1, source_target_pairs={{0,4},{4,0},{1,5},{5,1},{2,6},{6,2},{3,7},{7,3},{8,12},{12,8},{9,1... | collective-permute-start | bytes 1179656 | tf_op jit(solution)/shard_map/ppermute | solution.py:280
  169.3 3.4 %collective-permute-start.25 = (bf16[128,640]{1,0:T(8,128)(2,1)S(1)}, bf16[128,640]{1,0:T(8,128)(2,1)S(1)}, u32[]{:S(2)}, u32[]{:S(2)}) collective-permute-start(bf16[128,640]{1,0:T(8,128)(2,1)S(1)} %get-tuple-element.26), channel_id=1, source_target_pairs={{0,8},{8,0},{1,9},{9,1},{2,10},{10,2},{3,11},{11,3},{4,12},{12,4},... | collective-permute-start | bytes 491528 | tf_op jit(solution)/shard_map/ppermute | solution.py:280
  172.7 6.5 %collective-permute-done.26.rows = bf16[128,1280]{1,0:T(8,128)(2,1)S(1)} collective-permute-done((bf16[128,1280]{1,0:T(8,128)(2,1)S(1)}, bf16[128,1280]{1,0:T(8,128)(2,1)S(1)}, u32[]{:S(2)}, u32[]{:S(2)}) %collective-permute-start.26) | collective-permute-done | bytes 327712 | tf_op jit(solution)/shard_map/ppermute | solution.py:284
  (89 shorter events, 24.2 us)
Async XLA Ops:
  4.6 12.1 %collective-permute-start = (bf16[128,1280]{1,0:T(8,128)(2,1)S(1)}, bf16[128,1280]{1,0:T(8,128)(2,1)S(1)}, u32[]{:S(2)}, u32[]{:S(2)}) collective-permute-start(bf16[128,1280]{1,0:T(8,128)(2,1)S(1)} %fusion.28), channel_id=1, source_target_pairs={{0,32},{32,64},{64,96},{96,128},{128,160},{160,192},{192,224},{224... | collective-permute-start | bytes 983048 | tf_op jit(solution)/shard_map/ppermute | solution.py:284
  8.5 14.5 %collective-permute-start.5 = (bf16[40,2728]{1,0:T(8,128)(2,1)S(1)}, bf16[40,2728]{1,0:T(8,128)(2,1)S(1)}, u32[]{:S(2)}, u32[]{:S(2)}) collective-permute-start(bf16[40,2728]{1,0:T(8,128)(2,1)S(1)} %pad_maximum_fusion.1), channel_id=1, source_target_pairs={{0,32},{32,64},{64,96},{96,128},{128,160},{160,192},{192,224},{224... | collective-permute-start | bytes 654728 | tf_op jit(solution)/shard_map/ppermute | solution.py:284
  16.7 16.6 %collective-permute-start.1 = (bf16[128,1280]{1,0:T(8,128)(2,1)S(1)}, bf16[128,1280]{1,0:T(8,128)(2,1)S(1)}, u32[]{:S(2)}, u32[]{:S(2)}) collective-permute-start(bf16[128,1280]{1,0:T(8,128)(2,1)S(1)} %collective-permute-done), channel_id=1, source_target_pairs={{0,8},{8,0},{1,9},{9,1},{2,10},{10,2},{3,11},{11,3},{4,12},{12,4},... | collective-permute-start | bytes 983048 | tf_op jit(solution)/shard_map/ppermute | solution.py:280
  24.8 29.4 %all-to-all-start = ((bf16[4,40,896]{2,1,0:T(8,128)(2,1)}), bf16[4,40,896]{2,1,0:T(8,128)(2,1)S(1)}, u32[]{:S(2)}, u32[]{:S(2)}) async-start(bf16[4,40,896]{2,1,0:T(8,128)(2,1)} %fusion.38), calls=%async_computation | async-start | bytes 573440 | tf_op jit(solution)/shard_map/all_to_all | solution.py:319
  31.2 11.8 %collective-permute-start.15 = (bf16[80,1280]{1,0:T(8,128)(2,1)S(1)}, bf16[80,1280]{1,0:T(8,128)(2,1)S(1)}, u32[]{:S(2)}, u32[]{:S(2)}) collective-permute-start(bf16[80,1280]{1,0:T(8,128)(2,1)S(1)} %bitcast.42), channel_id=1, source_target_pairs={{0,32},{32,64},{64,96},{96,128},{128,160},{160,192},{192,224},{224... | collective-permute-start | bytes 614408 | tf_op jit(solution)/shard_map/ppermute | solution.py:284
  33.2 53.8 %copy-start = (f32[1,4,2688]{2,1,0:T(4,128)S(1)}, f32[1,4,2688]{2,1,0:T(4,128)}, u32[]{:S(2)}) copy-start(f32[1,4,2688]{2,1,0:T(4,128)} %all_taps.1) | copy-start | bytes 129028
  33.2 53.8 %copy-start.1 = (f32[1,2688]{1,0:T(1,128)S(1)}, f32[1,2688]{1,0:T(1,128)}, u32[]{:S(2)}) copy-start(f32[1,2688]{1,0:T(1,128)} %all_bias.1) | copy-start | bytes 32260
  34.2 78.5 %collective-permute-start.2 = (bf16[2,128,1280]{2,1,0:T(8,128)(2,1)}, bf16[2,128,1280]{2,1,0:T(8,128)(2,1)}, u32[]{:S(2)}, u32[]{:S(2)}) collective-permute-start(bf16[2,128,1280]{2,1,0:T(8,128)(2,1)} %pad_maximum_fusion), channel_id=1, source_target_pairs={{0,4},{4,0},{1,5},{5,1},{2,6},{6,2},{3,7},{7,3},{8,12},{12,8},{9,1... | collective-permute-start | bytes 1966088 | tf_op jit(solution)/shard_map/ppermute | solution.py:280
  43.0 19.3 %collective-permute-start.16 = (bf16[80,1280]{1,0:T(8,128)(2,1)S(1)}, bf16[80,1280]{1,0:T(8,128)(2,1)S(1)}, u32[]{:S(2)}, u32[]{:S(2)}) collective-permute-start(bf16[80,1280]{1,0:T(8,128)(2,1)S(1)} %collective-permute-done.15.rest_0_), channel_id=1, source_target_pairs={{0,16},{4,23},{16,1},{20,4},{1,17},{5,20},{17,2},{21,5},{2,18},{6,... | collective-permute-start | bytes 614408 | tf_op jit(solution)/shard_map/ppermute | solution.py:39
  54.2 14.1 %collective-permute-start.6 = (bf16[160,896]{1,0:T(8,128)(2,1)S(1)}, bf16[160,896]{1,0:T(8,128)(2,1)S(1)}, u32[]{:S(2)}, u32[]{:S(2)}) collective-permute-start(bf16[160,896]{1,0:T(8,128)(2,1)S(1)} %bitcast.33), channel_id=1, source_target_pairs={{0,16},{4,23},{16,1},{20,4},{1,17},{5,20},{17,2},{21,5},{2,18},{6,... | collective-permute-start | bytes 860168 | tf_op jit(solution)/shard_map/ppermute | solution.py:39
  57.3 17.3 %collective-permute-start.7 = (bf16[160,896]{1,0:T(8,128)(2,1)S(1)}, bf16[160,896]{1,0:T(8,128)(2,1)S(1)}, u32[]{:S(2)}, u32[]{:S(2)}) collective-permute-start(bf16[160,896]{1,0:T(8,128)(2,1)S(1)} %bitcast.34), channel_id=1, source_target_pairs={{0,19},{4,20},{16,0},{20,5},{1,16},{5,21},{17,1},{21,6},{2,17},{6,... | collective-permute-start | bytes 860168 | tf_op jit(solution)/shard_map/ppermute | solution.py:39
  60.4 18.2 %collective-permute-start.17 = (bf16[80,1280]{1,0:T(8,128)(2,1)S(1)}, bf16[80,1280]{1,0:T(8,128)(2,1)S(1)}, u32[]{:S(2)}, u32[]{:S(2)}) collective-permute-start(bf16[80,1280]{1,0:T(8,128)(2,1)S(1)} %collective-permute-done.15.rest_0_), channel_id=1, source_target_pairs={{0,19},{4,20},{16,0},{20,5},{1,16},{5,21},{17,1},{21,6},{2,17},{6,... | collective-permute-start | bytes 614408 | tf_op jit(solution)/shard_map/ppermute | solution.py:39
  62.3 22.6 %collective-permute-start.18 = (bf16[80,1280]{1,0:T(8,128)(2,1)S(1)}, bf16[80,1280]{1,0:T(8,128)(2,1)S(1)}, u32[]{:S(2)}, u32[]{:S(2)}) collective-permute-start(bf16[80,1280]{1,0:T(8,128)(2,1)S(1)} %collective-permute-done.16.rest_1_), channel_id=1, source_target_pairs={{0,16},{4,23},{16,1},{20,4},{1,17},{5,20},{17,2},{21,5},{2,18},{6,... | collective-permute-start | bytes 614408 | tf_op jit(solution)/shard_map/ppermute | solution.py:39
  68.3 33.2 %collective-permute-start.8 = (bf16[160,896]{1,0:T(8,128)(2,1)S(1)}, bf16[160,896]{1,0:T(8,128)(2,1)S(1)}, u32[]{:S(2)}, u32[]{:S(2)}) collective-permute-start(bf16[160,896]{1,0:T(8,128)(2,1)S(1)} %collective-permute-done.6.rest_1_), channel_id=1, source_target_pairs={{0,16},{4,23},{16,1},{20,4},{1,17},{5,20},{17,2},{21,5},{2,18},{6,... | collective-permute-start | bytes 860168 | tf_op jit(solution)/shard_map/ppermute | solution.py:39
  74.6 31.6 %collective-permute-start.9 = (bf16[160,896]{1,0:T(8,128)(2,1)S(1)}, bf16[160,896]{1,0:T(8,128)(2,1)S(1)}, u32[]{:S(2)}, u32[]{:S(2)}) collective-permute-start(bf16[160,896]{1,0:T(8,128)(2,1)S(1)} %collective-permute-done.7.rest_2_), channel_id=1, source_target_pairs={{0,19},{4,20},{16,0},{20,5},{1,16},{5,21},{17,1},{21,6},{2,17},{6,... | collective-permute-start | bytes 860168 | tf_op jit(solution)/shard_map/ppermute | solution.py:39
  78.6 18.3 %collective-permute-start.19 = (bf16[80,1280]{1,0:T(8,128)(2,1)S(1)}, bf16[80,1280]{1,0:T(8,128)(2,1)S(1)}, u32[]{:S(2)}, u32[]{:S(2)}) collective-permute-start(bf16[80,1280]{1,0:T(8,128)(2,1)S(1)} %collective-permute-done.17.rest_2_), channel_id=1, source_target_pairs={{0,19},{4,20},{16,0},{20,5},{1,16},{5,21},{17,1},{21,6},{2,17},{6,... | collective-permute-start | bytes 614408 | tf_op jit(solution)/shard_map/ppermute | solution.py:39
  85.0 13.8 %collective-permute-start.20 = (bf16[80,1280]{1,0:T(8,128)(2,1)S(1)}, bf16[80,1280]{1,0:T(8,128)(2,1)S(1)}, u32[]{:S(2)}, u32[]{:S(2)}) collective-permute-start(bf16[80,1280]{1,0:T(8,128)(2,1)S(1)} %collective-permute-done.18.rest_3_), channel_id=1, source_target_pairs={{0,16},{4,23},{16,1},{20,4},{1,17},{5,20},{17,2},{21,5},{2,18},{6,... | collective-permute-start | bytes 614408 | tf_op jit(solution)/shard_map/ppermute | solution.py:39
  96.8 41.9 %collective-permute-start.4 = (f32[16,768]{1,0:T(8,128)S(1)}, f32[16,768]{1,0:T(8,128)S(1)}, u32[]{:S(2)}, u32[]{:S(2)}) collective-permute-start(f32[16,768]{1,0:T(8,128)S(1)} %shard_map.109), channel_id=1, source_target_pairs={{0,32},{32,64},{64,96},{96,128},{128,160},{160,192},{192,224},{224... | collective-permute-start | bytes 147464 | tf_op jit(solution)/shard_map/ppermute | solution.py:284
  98.8 35.9 %collective-permute-start.21 = (bf16[80,1280]{1,0:T(8,128)(2,1)S(1)}, bf16[80,1280]{1,0:T(8,128)(2,1)S(1)}, u32[]{:S(2)}, u32[]{:S(2)}) collective-permute-start(bf16[80,1280]{1,0:T(8,128)(2,1)S(1)} %collective-permute-done.19.rest_4_), channel_id=1, source_target_pairs={{0,19},{4,20},{16,0},{20,5},{1,16},{5,21},{17,1},{21,6},{2,17},{6,... | collective-permute-start | bytes 614408 | tf_op jit(solution)/shard_map/ppermute | solution.py:39
  101.5 16.7 %collective-permute-start.10 = (bf16[160,896]{1,0:T(8,128)(2,1)S(1)}, bf16[160,896]{1,0:T(8,128)(2,1)S(1)}, u32[]{:S(2)}, u32[]{:S(2)}) collective-permute-start(bf16[160,896]{1,0:T(8,128)(2,1)S(1)} %collective-permute-done.8.rest_3_), channel_id=1, source_target_pairs={{0,16},{4,23},{16,1},{20,4},{1,17},{5,20},{17,2},{21,5},{2,18},{6,... | collective-permute-start | bytes 860168 | tf_op jit(solution)/shard_map/ppermute | solution.py:39
  106.2 23.6 %collective-permute-start.11 = (bf16[160,896]{1,0:T(8,128)(2,1)S(1)}, bf16[160,896]{1,0:T(8,128)(2,1)S(1)}, u32[]{:S(2)}, u32[]{:S(2)}) collective-permute-start(bf16[160,896]{1,0:T(8,128)(2,1)S(1)} %collective-permute-done.9.rest_4_), channel_id=1, source_target_pairs={{0,19},{4,20},{16,0},{20,5},{1,16},{5,21},{17,1},{21,6},{2,17},{6,... | collective-permute-start | bytes 860168 | tf_op jit(solution)/shard_map/ppermute | solution.py:39
  118.2 22.7 %collective-permute-start.12 = (bf16[80,896]{1,0:T(8,128)(2,1)S(1)}, bf16[80,896]{1,0:T(8,128)(2,1)S(1)}, u32[]{:S(2)}, u32[]{:S(2)}) collective-permute-start(bf16[80,896]{1,0:T(8,128)(2,1)S(1)} %slice.39), channel_id=1, source_target_pairs={{0,16},{4,23},{16,1},{20,4},{1,17},{5,20},{17,2},{21,5},{2,18},{6,... | collective-permute-start | bytes 430088 | tf_op jit(solution)/shard_map/ppermute | solution.py:39
  129.8 11.8 %collective-permute-start.13 = (bf16[80,896]{1,0:T(8,128)(2,1)S(1)}, bf16[80,896]{1,0:T(8,128)(2,1)S(1)}, u32[]{:S(2)}, u32[]{:S(2)}) collective-permute-start(bf16[80,896]{1,0:T(8,128)(2,1)S(1)} %slice.40), channel_id=1, source_target_pairs={{0,19},{4,20},{16,0},{20,5},{1,16},{5,21},{17,1},{21,6},{2,17},{6,... | collective-permute-start | bytes 430088 | tf_op jit(solution)/shard_map/ppermute | solution.py:39
  132.0 8.9 %collective-permute-start.3 = (bf16[8,1280]{1,0:T(8,128)(2,1)S(1)}, bf16[8,1280]{1,0:T(8,128)(2,1)S(1)}, u32[]{:S(2)}, u32[]{:S(2)}) collective-permute-start(bf16[8,1280]{1,0:T(8,128)(2,1)S(1)} %slice.35), channel_id=1, source_target_pairs={{0,16},{1,17},{2,18},{3,19},{4,20},{5,21},{6,22},{7,23},{8,24},{9,... | collective-permute-start | bytes 61448 | tf_op jit(solution)/shard_map/ppermute | solution.py:335
  134.7 20.0 %collective-permute-start.22 = (bf16[80,640]{1,0:T(8,128)(2,1)S(1)}, bf16[80,640]{1,0:T(8,128)(2,1)S(1)}, u32[]{:S(2)}, u32[]{:S(2)}) collective-permute-start(bf16[80,640]{1,0:T(8,128)(2,1)S(1)} %slice.41), channel_id=1, source_target_pairs={{0,16},{4,23},{16,1},{20,4},{1,17},{5,20},{17,2},{21,5},{2,18},{6,... | collective-permute-start | bytes 307208 | tf_op jit(solution)/shard_map/ppermute | solution.py:39
  138.8 15.9 %collective-permute-start.23 = (bf16[80,640]{1,0:T(8,128)(2,1)S(1)}, bf16[80,640]{1,0:T(8,128)(2,1)S(1)}, u32[]{:S(2)}, u32[]{:S(2)}) collective-permute-start(bf16[80,640]{1,0:T(8,128)(2,1)S(1)} %slice.42), channel_id=1, source_target_pairs={{0,19},{4,20},{16,0},{20,5},{1,16},{5,21},{17,1},{21,6},{2,17},{6,... | collective-permute-start | bytes 307208 | tf_op jit(solution)/shard_map/ppermute | solution.py:39
  149.2 7.0 %collective-permute-start.14 = (bf16[64,640]{1,0:T(8,128)(2,1)S(1)}, bf16[64,640]{1,0:T(8,128)(2,1)S(1)}, u32[]{:S(2)}, u32[]{:S(2)}) collective-permute-start(bf16[64,640]{1,0:T(8,128)(2,1)S(1)} %get-tuple-element.22), channel_id=1, source_target_pairs={{0,16},{1,17},{2,18},{3,19},{4,20},{5,21},{6,22},{7,23},{8,24},{9,... | collective-permute-start | bytes 245768 | tf_op jit(solution)/shard_map/ppermute | solution.py:367
  158.6 8.5 %collective-permute-start.27 = (bf16[2,128,768]{2,1,0:T(8,128)(2,1)S(1)}, bf16[2,128,768]{2,1,0:T(8,128)(2,1)S(1)}, u32[]{:S(2)}, u32[]{:S(2)}) collective-permute-start(bf16[2,128,768]{2,1,0:T(8,128)(2,1)S(1)} %get-tuple-element.28), channel_id=1, source_target_pairs={{0,4},{4,0},{1,5},{5,1},{2,6},{6,2},{3,7},{7,3},{8,12},{12,8},{9,1... | collective-permute-start | bytes 1179656 | tf_op jit(solution)/shard_map/ppermute | solution.py:280
  163.2 6.0 %collective-permute-start.24 = (bf16[2,128,640]{2,1,0:T(8,128)(2,1)S(1)}, bf16[2,128,640]{2,1,0:T(8,128)(2,1)S(1)}, u32[]{:S(2)}, u32[]{:S(2)}) collective-permute-start(bf16[2,128,640]{2,1,0:T(8,128)(2,1)S(1)} %get-tuple-element.24), channel_id=1, source_target_pairs={{0,4},{4,0},{1,5},{5,1},{2,6},{6,2},{3,7},{7,3},{8,12},{12,8},{9,1... | collective-permute-start | bytes 983048 | tf_op jit(solution)/shard_map/ppermute | solution.py:280
  165.1 14.0 %collective-permute-start.26 = (bf16[128,1280]{1,0:T(8,128)(2,1)S(1)}, bf16[128,1280]{1,0:T(8,128)(2,1)S(1)}, u32[]{:S(2)}, u32[]{:S(2)}) collective-permute-start(bf16[128,1280]{1,0:T(8,128)(2,1)S(1)} %bitcast.37), channel_id=1, source_target_pairs={{0,32},{32,64},{64,96},{96,128},{128,160},{160,192},{192,224},{224... | collective-permute-start | bytes 983048 | tf_op jit(solution)/shard_map/ppermute | solution.py:284
  167.3 11.9 %collective-permute-start.28 = (bf16[128,768]{1,0:T(8,128)(2,1)S(1)}, bf16[128,768]{1,0:T(8,128)(2,1)S(1)}, u32[]{:S(2)}, u32[]{:S(2)}) collective-permute-start(bf16[128,768]{1,0:T(8,128)(2,1)S(1)} %get-tuple-element.30), channel_id=1, source_target_pairs={{0,8},{8,0},{1,9},{9,1},{2,10},{10,2},{3,11},{11,3},{4,12},{12,4},... | collective-permute-start | bytes 589832 | tf_op jit(solution)/shard_map/ppermute | solution.py:280
  169.3 10.0 %collective-permute-start.25 = (bf16[128,640]{1,0:T(8,128)(2,1)S(1)}, bf16[128,640]{1,0:T(8,128)(2,1)S(1)}, u32[]{:S(2)}, u32[]{:S(2)}) collective-permute-start(bf16[128,640]{1,0:T(8,128)(2,1)S(1)} %get-tuple-element.26), channel_id=1, source_target_pairs={{0,8},{8,0},{1,9},{9,1},{2,10},{10,2},{3,11},{11,3},{4,12},{12,4},... | collective-permute-start | bytes 491528 | tf_op jit(solution)/shard_map/ppermute | solution.py:280
  (8 other events, 245.6 us)
where the time goes:
time: 181 us; the launch traced here: 180 us
  starting transfers between devices  122 us (67%)
  waiting for transfers between devices  36.4 us (20%)
  Pallas kernels  12 us (7%)
  other arithmetic  4.99 us (3%)
  matrix products  2.6 us (1%)
    ppermute x16, starting transfers between devices, shifted(): return lax.ppermute(x, RING, pairs)  74.7 us
    ppermute x6, starting transfers between devices, swapped(): return lax.ppermute(x, axis, [(0, 1), (1, 0)])  20.1 us
    ppermute x5, waiting for transfers between devices, onward(): return lax.ppermute(x, 'section', [(i, (i + 1) % 16) for i in range(16)])  18.3 us
    ppermute x16, waiting for transfers between devices, shifted(): return lax.ppermute(x, RING, pairs)  16.5 us
    ppermute x5, starting transfers between devices, onward(): return lax.ppermute(x, 'section', [(i, (i + 1) % 16) for i in range(16)])  12.8 us
    pallas_call x7, Pallas kernels, called(): pl.pallas_call(kernel, out_shape=outs, in_specs=[SMEM] * len(scalars) + [...  12 us
    all_to_all x1, starting transfers between devices, shards(): classes = lax.all_to_all(packed, ('par', 'core'), 0, 0).reshape(160, WIDE)  6.46 us
    ppermute x1, starting transfers between devices, shards(): arriving = lax.ppermute(state, 'blk', [(0, 1)])  5.5 us
  transfers between devices with their start and end apart: 30, of which 9 were waited for; matrix products, arithmetic and copies ran while one was open for 2% of the time, Pallas kernels for 5%

commit v1 on v0

--- a/solution.py
+++ b/solution.py
@@ -250,15 +250,14 @@
     square = jnp.sum(total[:, HALF:], axis=1, keepdims=True)
     scale = lax.rsqrt(square * (1.0 / INNER) + epsilon)
     scale_out[...] = jnp.broadcast_to(scale, (BLOCK, 128))
-    wide = rows[:, :HALF].astype(jnp.float32)
+    wide = rows[0, 0, :, :HALF].astype(jnp.float32)
     out[...] = (wide + total[:, :HALF] * scale).astype(jnp.bfloat16)
 
 
-def second_kernel(keep, came, rows, scale, first, out):
+def second_kernel(keep, came, rows, scale, out):
     total = keep[...] + came[...].astype(jnp.float32)
-    wide = rows[:, HALF:].astype(jnp.float32)
-    out[0, 0, :, :HALF] = first[...]
-    out[0, 0, :, HALF:] = (wide + total * scale[:, :1]).astype(jnp.bfloat16)
+    wide = rows[0, 0, :, HALF:].astype(jnp.float32)
+    out[...] = (wide + total * scale[:, :1]).astype(jnp.bfloat16)
 
 
 VMEM = pl.BlockSpec(memory_space=pltpu.VMEM)
@@ -278,10 +277,6 @@
 
 def swapped(x, axis):
     return lax.ppermute(x, axis, [(0, 1), (1, 0)])
-
-
-def onward(x):
-    return lax.ppermute(x, "section", [(i, (i + 1) % 16) for i in range(16)])
 
 
 def both_of(mine, theirs, index):
@@ -308,9 +303,8 @@
     place = lax.axis_index("dp") * 2 + lax.axis_index("blk")
     where = jnp.stack([place, 1 - 2 * core, group, par, core]).astype(jnp.int32)
 
-    out_chunks = gathered(onward(w_out[0]), 1)
-    raw = onward(jnp.concatenate([w_xbc[0], w_dt[0]], axis=1))
-    xbc, dtw = raw[:, : INNER + 2 * STATE], raw[:, INNER + 2 * STATE :]
+    out_chunks = gathered(w_out[0], 1)
+    xbc, dtw = w_xbc[0], w_dt[0]
     inner = xbc[:, :INNER].reshape(40, 2, 4, 320).transpose(2, 0, 1, 3).reshape(4, 40, LOCAL)
     shared = jnp.broadcast_to(xbc[None, :, INNER:], (4, 40, 2 * STATE))
     steps = dtw.reshape(40, 2, 4, 5).transpose(2, 0, 1, 3).reshape(4, 40, LOCAL_HEADS)
@@ -328,8 +322,8 @@
     source = (target // 640) * 640 + (target // 40 % 4) * 160 + (target // 160 % 4) * 40 + target % 40
     select = (feature == source).astype(jnp.bfloat16)
     normed = jnp.dot(normed, select, preferred_element_type=jnp.float32).astype(jnp.bfloat16)
-    normed = onward(normed)
-    pair = both_of(normed, swapped(normed, "par"), par)
+    beside = swapped(normed, "par")
+    pair = both_of(normed, beside, par)
     quad = both_of(pair, swapped(pair, "core"), core)
     rows = quad.transpose(1, 0, 2, 3).reshape(ROWS, D)
     halo = lax.ppermute(rows[ROWS - 8 :], "blk", [(0, 1)])
@@ -347,8 +341,6 @@
         skip_weight,
         inner_gain,
     )
-    params = onward(params)
-    residual = onward(rows_in)
     y_local, c_rows, grown, state = called(
         mix_kernel,
         (
@@ -406,19 +398,16 @@
         (),
         keep_x,
         came_x,
-        residual,
-    )
-    return called(
-        second_kernel,
-        shape((1, 1, BLOCK, D), bf16),
-        [],
-        (),
-        keep_y,
-        came_y,
-        residual,
-        scale,
-        next_x,
-    )
+        stream,
+    )
+    next_y = called(
+        second_kernel, shape((BLOCK, HALF), bf16), [], (), keep_y, came_y, stream, scale
+    )
+    onward = [(i, (i + 1) % 16) for i in range(16)]
+    moved_x = lax.ppermute(next_x, "section", onward)
+    moved_y = lax.ppermute(next_y, "section", onward)
+    moved = jnp.concatenate([moved_x, moved_y], axis=1)
+    return moved[None, None]
 
 
 def solution(mesh):

time: 181 us -> 178 us (0.983)
  the two profiles are of different devices: /device:TPU:1 before, /device:TPU:64 now
where the time goes in v1:
time: 178 us; the launch traced here: 177 us
  starting transfers between devices  104 us (58%)
  waiting for transfers between devices  40.7 us (23%)
  Pallas kernels  12.2 us (7%)
  local copies, waits for them, and re-layouts  10.7 us (6%)
  other arithmetic  5.66 us (3%)
  matrix products  2.6 us (1%)
    ppermute x16, starting transfers between devices, shifted(): return lax.ppermute(x, RING, pairs)  73.4 us
    ppermute x16, waiting for transfers between devices, shifted(): return lax.ppermute(x, RING, pairs)  18.1 us
    ppermute x6, starting transfers between devices, swapped(): return lax.ppermute(x, axis, [(0, 1), (1, 0)])  17.7 us
    pallas_call x7, Pallas kernels, called(): pl.pallas_call(kernel, out_shape=outs, in_specs=[SMEM] * len(scalars) + [...  12.2 us
    ppermute x6, waiting for transfers between devices, swapped(): return lax.ppermute(x, axis, [(0, 1), (1, 0)])  8.91 us
    ppermute x1, waiting for transfers between devices, shards(): arriving = lax.ppermute(state, 'blk', [(0, 1)])  6.32 us
    unnamed x42, local copies, waits for them, and re-layouts  6.02 us
    ppermute x1, waiting for transfers between devices, shards(): moved_y = lax.ppermute(next_y, 'section', onward)  4.31 us
  transfers between devices with their start and end apart: 27, of which 10 were waited for; matrix products, arithmetic and copies ran while one was open for 4% of the time, Pallas kernels for 5%

profile of v1, /device:TPU:64, one launch (start us, length us, event | category | flops | bytes accessed | tf_op | source)
XLA Modules:
  0.0 176.9 jit_solution(2230410943220357955)
XLA Ops:
  1.9 2.6 %fusion.28 = bf16[128,1280]{1,0:T(8,128)(2,1)S(1)} fusion(s32[1280]{0:T(1024)S(1)} %get-tuple-element.39, s32[1280]{0:T(1024)S(1)} %get-tuple-element.41, s32[1280]{0:T(1024)S(1)} %get-tuple-element.37, s32[1280]{0:T(1024)S(1)} %get-tuple-element.42, s32[1280]{0:T(1024)S(1)} %get-tuple-element.38, s32[1280]{0:T(1024)S(1)} %get-tuple-element.47, ...), kind=kOutput, calls=%fused_computation.37 | convolution fusion | flops 474316800 | bytes 707072 | tf_op jit(solution)/shard_map/dot_general | solution.py:324
  4.6 3.8 %collective-permute-start = (bf16[128,1280]{1,0:T(8,128)(2,1)S(1)}, bf16[128,1280]{1,0:T(8,128)(2,1)S(1)}, u32[]{:S(2)}, u32[]{:S(2)}) collective-permute-start(bf16[128,1280]{1,0:T(8,128)(2,1)S(1)} %fusion.28), channel_id=1, source_target_pairs={{0,8},{8,0},{1,9},{9,1},{2,10},{10,2},{3,11},{11,3},{4,12},{12,4},... | collective-permute-start | bytes 983048 | tf_op jit(solution)/shard_map/ppermute | solution.py:279
  10.1 3.5 %all-to-all-start = ((bf16[4,40,896]{2,1,0:T(8,128)(2,1)}), bf16[4,40,896]{2,1,0:T(8,128)(2,1)S(1)}, u32[]{:S(2)}, u32[]{:S(2)}) async-start(bf16[4,40,896]{2,1,0:T(8,128)(2,1)} %fusion.39), calls=%async_computation | async-start | bytes 573440 | tf_op jit(solution)/shard_map/all_to_all | solution.py:313
  13.6 2.5 %collective-permute-done = bf16[128,1280]{1,0:T(8,128)(2,1)S(1)} collective-permute-done((bf16[128,1280]{1,0:T(8,128)(2,1)S(1)}, bf16[128,1280]{1,0:T(8,128)(2,1)S(1)}, u32[]{:S(2)}, u32[]{:S(2)}) %collective-permute-start) | collective-permute-done | bytes 327712 | tf_op jit(solution)/shard_map/ppermute | solution.py:279
  19.0 6.4 %collective-permute-start.12 = (bf16[80,1280]{1,0:T(8,128)(2,1)S(1)}, bf16[80,1280]{1,0:T(8,128)(2,1)S(1)}, u32[]{:S(2)}, u32[]{:S(2)}) collective-permute-start(bf16[80,1280]{1,0:T(8,128)(2,1)S(1)} %bitcast.38), channel_id=1, source_target_pairs={{0,16},{4,23},{16,1},{20,4},{1,17},{5,20},{17,2},{21,5},{2,18},{6,... | collective-permute-start | bytes 614408 | tf_op jit(solution)/shard_map/ppermute | solution.py:39
  27.3 6.0 %collective-permute-start.3 = (bf16[160,896]{1,0:T(8,128)(2,1)S(1)}, bf16[160,896]{1,0:T(8,128)(2,1)S(1)}, u32[]{:S(2)}, u32[]{:S(2)}) collective-permute-start(bf16[160,896]{1,0:T(8,128)(2,1)S(1)} %bitcast.36), channel_id=1, source_target_pairs={{0,16},{4,23},{16,1},{20,4},{1,17},{5,20},{17,2},{21,5},{2,18},{6,... | collective-permute-start | bytes 860168 | tf_op jit(solution)/shard_map/ppermute | solution.py:39
  33.4 2.8 %collective-permute-start.13 = (bf16[80,1280]{1,0:T(8,128)(2,1)S(1)}, bf16[80,1280]{1,0:T(8,128)(2,1)S(1)}, u32[]{:S(2)}, u32[]{:S(2)}) collective-permute-start(bf16[80,1280]{1,0:T(8,128)(2,1)S(1)} %bitcast.39), channel_id=1, source_target_pairs={{0,19},{4,20},{16,0},{20,5},{1,16},{5,21},{17,1},{21,6},{2,17},{6,... | collective-permute-start | bytes 614408 | tf_op jit(solution)/shard_map/ppermute | solution.py:39
  36.2 5.2 %collective-permute-start.14 = (bf16[80,1280]{1,0:T(8,128)(2,1)S(1)}, bf16[80,1280]{1,0:T(8,128)(2,1)S(1)}, u32[]{:S(2)}, u32[]{:S(2)}) collective-permute-start(bf16[80,1280]{1,0:T(8,128)(2,1)S(1)} %collective-permute-done.12.rest_1_), channel_id=1, source_target_pairs={{0,16},{4,23},{16,1},{20,4},{1,17},{5,20},{17,2},{21,5},{2,18},{6,... | collective-permute-start | bytes 614408 | tf_op jit(solution)/shard_map/ppermute | solution.py:39
  41.4 2.0 %collective-permute-done.4.rest_2_ = bf16[160,896]{1,0:T(8,128)(2,1)S(1)} collective-permute-done((bf16[160,896]{1,0:T(8,128)(2,1)S(1)}, bf16[160,896]{1,0:T(8,128)(2,1)S(1)}, u32[]{:S(2)}, u32[]{:S(2)}) %collective-permute-start.4) | collective-permute-done | bytes 286752 | tf_op jit(solution)/shard_map/ppermute | solution.py:39
  43.3 3.9 %collective-permute-start.6 = (bf16[160,896]{1,0:T(8,128)(2,1)S(1)}, bf16[160,896]{1,0:T(8,128)(2,1)S(1)}, u32[]{:S(2)}, u32[]{:S(2)}) collective-permute-start(bf16[160,896]{1,0:T(8,128)(2,1)S(1)} %collective-permute-done.4.rest_2_), channel_id=1, source_target_pairs={{0,19},{4,20},{16,0},{20,5},{1,16},{5,21},{17,1},{21,6},{2,17},{6,... | collective-permute-start | bytes 860168 | tf_op jit(solution)/shard_map/ppermute | solution.py:39
  47.2 5.4 %collective-permute-start.5 = (bf16[160,896]{1,0:T(8,128)(2,1)S(1)}, bf16[160,896]{1,0:T(8,128)(2,1)S(1)}, u32[]{:S(2)}, u32[]{:S(2)}) collective-permute-start(bf16[160,896]{1,0:T(8,128)(2,1)S(1)} %collective-permute-done.3.rest_1_), channel_id=1, source_target_pairs={{0,16},{4,23},{16,1},{20,4},{1,17},{5,20},{17,2},{21,5},{2,18},{6,... | collective-permute-start | bytes 860168 | tf_op jit(solution)/shard_map/ppermute | solution.py:39
  53.3 3.9 %collective-permute-start.15 = (bf16[80,1280]{1,0:T(8,128)(2,1)S(1)}, bf16[80,1280]{1,0:T(8,128)(2,1)}, u32[]{:S(2)}, u32[]{:S(2)}) collective-permute-start(bf16[80,1280]{1,0:T(8,128)(2,1)S(1)} %collective-permute-done.13.rest_2_), channel_id=1, source_target_pairs={{0,19},{4,20},{16,0},{20,5},{1,16},{5,21},{17,1},{21,6},{2,17},{6,... | collective-permute-start | bytes 614408 | tf_op jit(solution)/shard_map/ppermute | solution.py:39
  57.9 4.4 %collective-permute-start.16 = (bf16[80,1280]{1,0:T(8,128)(2,1)S(1)}, bf16[80,1280]{1,0:T(8,128)(2,1)S(1)}, u32[]{:S(2)}, u32[]{:S(2)}) collective-permute-start(bf16[80,1280]{1,0:T(8,128)(2,1)S(1)} %collective-permute-done.14.rest_3_), channel_id=1, source_target_pairs={{0,16},{4,23},{16,1},{20,4},{1,17},{5,20},{17,2},{21,5},{2,18},{6,... | collective-permute-start | bytes 614408 | tf_op jit(solution)/shard_map/ppermute | solution.py:39
  62.3 11.3 %collective-permute-done.15.rest_4_ = bf16[80,1280]{1,0:T(8,128)(2,1)} collective-permute-done((bf16[80,1280]{1,0:T(8,128)(2,1)S(1)}, bf16[80,1280]{1,0:T(8,128)(2,1)}, u32[]{:S(2)}, u32[]{:S(2)}) %collective-permute-start.15) | collective-permute-done | bytes 204832 | tf_op jit(solution)/shard_map/ppermute | solution.py:39
  73.6 4.1 %collective-permute-start.17 = (bf16[80,1280]{1,0:T(8,128)(2,1)}, bf16[80,1280]{1,0:T(8,128)(2,1)S(1)}, u32[]{:S(2)}, u32[]{:S(2)}) collective-permute-start(bf16[80,1280]{1,0:T(8,128)(2,1)} %collective-permute-done.15.rest_4_), channel_id=1, source_target_pairs={{0,19},{4,20},{16,0},{20,5},{1,16},{5,21},{17,1},{21,6},{2,17},{6,... | collective-permute-start | bytes 614408 | tf_op jit(solution)/shard_map/ppermute | solution.py:39
  78.4 6.7 %collective-permute-start.8 = (bf16[160,896]{1,0:T(8,128)(2,1)S(1)}, bf16[160,896]{1,0:T(8,128)(2,1)S(1)}, u32[]{:S(2)}, u32[]{:S(2)}) collective-permute-start(bf16[160,896]{1,0:T(8,128)(2,1)S(1)} %collective-permute-done.6.rest_4_), channel_id=1, source_target_pairs={{0,19},{4,20},{16,0},{20,5},{1,16},{5,21},{17,1},{21,6},{2,17},{6,... | collective-permute-start | bytes 860168 | tf_op jit(solution)/shard_map/ppermute | solution.py:39
  88.3 4.1 %collective-permute-done.8.rest_6_ = bf16[160,896]{1,0:T(8,128)(2,1)S(1)} collective-permute-done((bf16[160,896]{1,0:T(8,128)(2,1)S(1)}, bf16[160,896]{1,0:T(8,128)(2,1)S(1)}, u32[]{:S(2)}, u32[]{:S(2)}) %collective-permute-start.8) | collective-permute-done | bytes 286752 | tf_op jit(solution)/shard_map/ppermute | solution.py:39
  93.1 9.9 %collective-permute-start.10 = (bf16[80,896]{1,0:T(8,128)(2,1)}, bf16[80,896]{1,0:T(8,128)(2,1)}, u32[]{:S(2)}, u32[]{:S(2)}) collective-permute-start(bf16[80,896]{1,0:T(8,128)(2,1)} %slice.32), channel_id=1, source_target_pairs={{0,19},{4,20},{16,0},{20,5},{1,16},{5,21},{17,1},{21,6},{2,17},{6,... | collective-permute-start | bytes 430088 | tf_op jit(solution)/shard_map/ppermute | solution.py:39
  107.8 5.6 %collective-permute-start.18 = (bf16[80,640]{1,0:T(8,128)(2,1)}, bf16[80,640]{1,0:T(8,128)(2,1)S(1)}, u32[]{:S(2)}, u32[]{:S(2)}) collective-permute-start(bf16[80,640]{1,0:T(8,128)(2,1)} %slice.33), channel_id=1, source_target_pairs={{0,16},{4,23},{16,1},{20,4},{1,17},{5,20},{17,2},{21,5},{2,18},{6,... | collective-permute-start | bytes 307208 | tf_op jit(solution)/shard_map/ppermute | solution.py:39
  114.0 3.4 %collective-permute-start.19 = (bf16[80,640]{1,0:T(8,128)(2,1)}, bf16[80,640]{1,0:T(8,128)(2,1)}, u32[]{:S(2)}, u32[]{:S(2)}) collective-permute-start(bf16[80,640]{1,0:T(8,128)(2,1)} %slice.34), channel_id=1, source_target_pairs={{0,19},{4,20},{16,0},{20,5},{1,16},{5,21},{17,1},{21,6},{2,17},{6,... | collective-permute-start | bytes 307208 | tf_op jit(solution)/shard_map/ppermute | solution.py:39
  124.0 8.1 %shard_map.110 = (f32[512,640]{1,0:T(8,128)S(1)}, bf16[512,64]{1,0:T(8,128)(2,1)S(1)}, f32[512,640]{1,0:T(8,128)S(1)}, bf16[64,640]{1,0:T(8,128)(2,1)S(1)}) custom-call(s32[5]{0:T(128)S(1)} %copy-done.14, bf16[512,1280]{1,0:T(8,128)(2,1)S(1)} %bitcast.34, bf16[8,1280]{1,0:T(8,128)(2,1)} %collective-permute-done.2.halo, f32[16,768]{1,0:T(8,128)S(1)} %shard_map.109.params, ...), custom_call_target="tpu_custom_call" | custom-call | tf_op jit(solution)/shard_map/pallas_call | solution.py:268
  133.6 6.3 %collective-permute-done.11.arriving = bf16[64,640]{1,0:T(8,128)(2,1)S(1)} collective-permute-done((bf16[64,640]{1,0:T(8,128)(2,1)S(1)}, bf16[64,640]{1,0:T(8,128)(2,1)S(1)}, u32[]{:S(2)}, u32[]{:S(2)}) %collective-permute-start.11) | collective-permute-done | bytes 81952 | tf_op jit(solution)/shard_map/ppermute | solution.py:359
  139.9 2.9 %shard_map.111 = (f32[2,128,768]{2,1,0:T(8,128)S(1)}, bf16[2,128,768]{2,1,0:T(8,128)(2,1)S(1)}, f32[2,128,640]{2,1,0:T(8,128)S(1)}, bf16[2,128,640]{2,1,0:T(8,128)(2,1)S(1)}) custom-call(s32[5]{0:T(128)S(1)} %copy-done.14, f32[512,640]{1,0:T(8,128)S(1)} %get-tuple-element.19.y_in, bf16[512,64]{1,0:T(8,128)(2,1)S(1)} %get-tuple-element.20.c_in, ...), custom_call_target="tpu_custom_call" | custom-call | tf_op jit(solution)/shard_map/pallas_call | solution.py:268
  142.8 2.1 %collective-permute-start.20 = (bf16[2,128,768]{2,1,0:T(8,128)(2,1)S(1)}, bf16[2,128,768]{2,1,0:T(8,128)(2,1)S(1)}, u32[]{:S(2)}, u32[]{:S(2)}) collective-permute-start(bf16[2,128,768]{2,1,0:T(8,128)(2,1)S(1)} %get-tuple-element.24), channel_id=1, source_target_pairs={{0,4},{4,0},{1,5},{5,1},{2,6},{6,2},{3,7},{7,3},{8,12},{12,8},{9,1... | collective-permute-start | bytes 1179656 | tf_op jit(solution)/shard_map/ppermute | solution.py:279
  144.9 2.4 %collective-permute-start.23 = (bf16[2,128,640]{2,1,0:T(8,128)(2,1)S(1)}, bf16[2,128,640]{2,1,0:T(8,128)(2,1)S(1)}, u32[]{:S(2)}, u32[]{:S(2)}) collective-permute-start(bf16[2,128,640]{2,1,0:T(8,128)(2,1)S(1)} %get-tuple-element.29), channel_id=1, source_target_pairs={{0,4},{4,0},{1,5},{5,1},{2,6},{6,2},{3,7},{7,3},{8,12},{12,8},{9,1... | collective-permute-start | bytes 983048 | tf_op jit(solution)/shard_map/ppermute | solution.py:279
  147.5 5.6 %collective-permute-start.21 = (bf16[128,768]{1,0:T(8,128)(2,1)S(1)}, bf16[128,768]{1,0:T(8,128)(2,1)S(1)}, u32[]{:S(2)}, u32[]{:S(2)}) collective-permute-start(bf16[128,768]{1,0:T(8,128)(2,1)S(1)} %get-tuple-element.26), channel_id=1, source_target_pairs={{0,8},{8,0},{1,9},{9,1},{2,10},{10,2},{3,11},{11,3},{4,12},{12,4},... | collective-permute-start | bytes 589832 | tf_op jit(solution)/shard_map/ppermute | solution.py:279
  155.2 3.7 %collective-permute-done.21.came = bf16[128,768]{1,0:T(8,128)(2,1)S(1)} collective-permute-done((bf16[128,768]{1,0:T(8,128)(2,1)S(1)}, bf16[128,768]{1,0:T(8,128)(2,1)S(1)}, u32[]{:S(2)}, u32[]{:S(2)}) %collective-permute-start.21) | collective-permute-done | bytes 196640 | tf_op jit(solution)/shard_map/ppermute | solution.py:279
  159.0 2.7 %collective-permute-done.24.came = bf16[128,640]{1,0:T(8,128)(2,1)S(1)} collective-permute-done((bf16[128,640]{1,0:T(8,128)(2,1)S(1)}, bf16[128,640]{1,0:T(8,128)(2,1)S(1)}, u32[]{:S(2)}, u32[]{:S(2)}) %collective-permute-start.24) | collective-permute-done | bytes 163872 | tf_op jit(solution)/shard_map/ppermute | solution.py:279
  161.8 3.4 %collective-permute-start.25 = (bf16[128,640]{1,0:T(8,128)(2,1)S(1)}, bf16[128,640]{1,0:T(8,128)(2,1)S(1)}, u32[]{:S(2)}, u32[]{:S(2)}) collective-permute-start(bf16[128,640]{1,0:T(8,128)(2,1)S(1)} %shard_map.115), channel_id=1, source_target_pairs={{0,32},{32,64},{64,96},{96,128},{128,160},{160,192},{192,224},{224... | collective-permute-start | bytes 491528 | tf_op jit(solution)/shard_map/ppermute | solution.py:408
  165.2 3.6 %collective-permute-start.22 = (bf16[128,640]{1,0:T(8,128)(2,1)S(1)}, bf16[128,640]{1,0:T(8,128)(2,1)S(1)}, u32[]{:S(2)}, u32[]{:S(2)}) collective-permute-start(bf16[128,640]{1,0:T(8,128)(2,1)S(1)} %get-tuple-element.27), channel_id=1, source_target_pairs={{0,32},{32,64},{64,96},{96,128},{128,160},{160,192},{192,224},{224... | collective-permute-start | bytes 491528 | tf_op jit(solution)/shard_map/ppermute | solution.py:407
  168.9 4.3 %collective-permute-done.25 = bf16[128,640]{1,0:T(8,128)(2,1)S(1)} collective-permute-done((bf16[128,640]{1,0:T(8,128)(2,1)S(1)}, bf16[128,640]{1,0:T(8,128)(2,1)S(1)}, u32[]{:S(2)}, u32[]{:S(2)}) %collective-permute-start.25) | collective-permute-done | bytes 163872 | tf_op jit(solution)/shard_map/ppermute | solution.py:408
  173.2 3.0 %collective-permute-done.22 = bf16[128,640]{1,0:T(8,128)(2,1)S(1)} collective-permute-done((bf16[128,640]{1,0:T(8,128)(2,1)S(1)}, bf16[128,640]{1,0:T(8,128)(2,1)S(1)}, u32[]{:S(2)}, u32[]{:S(2)}) %collective-permute-start.22) | collective-permute-done | bytes 163872 | tf_op jit(solution)/shard_map/ppermute | solution.py:407
  (102 shorter events, 30.7 us)
Async XLA Ops:
  4.6 11.5 %collective-permute-start = (bf16[128,1280]{1,0:T(8,128)(2,1)S(1)}, bf16[128,1280]{1,0:T(8,128)(2,1)S(1)}, u32[]{:S(2)}, u32[]{:S(2)}) collective-permute-start(bf16[128,1280]{1,0:T(8,128)(2,1)S(1)} %fusion.28), channel_id=1, source_target_pairs={{0,8},{8,0},{1,9},{9,1},{2,10},{10,2},{3,11},{11,3},{4,12},{12,4},... | collective-permute-start | bytes 983048 | tf_op jit(solution)/shard_map/ppermute | solution.py:279
  10.1 15.3 %all-to-all-start = ((bf16[4,40,896]{2,1,0:T(8,128)(2,1)}), bf16[4,40,896]{2,1,0:T(8,128)(2,1)S(1)}, u32[]{:S(2)}, u32[]{:S(2)}) async-start(bf16[4,40,896]{2,1,0:T(8,128)(2,1)} %fusion.39), calls=%async_computation | async-start | bytes 573440 | tf_op jit(solution)/shard_map/all_to_all | solution.py:313
  17.1 70.0 %collective-permute-start.1 = (bf16[2,128,1280]{2,1,0:T(8,128)(2,1)}, bf16[2,128,1280]{2,1,0:T(8,128)(2,1)}, u32[]{:S(2)}, u32[]{:S(2)}) collective-permute-start(bf16[2,128,1280]{2,1,0:T(8,128)(2,1)} %pad_maximum_fusion), channel_id=1, source_target_pairs={{0,4},{4,0},{1,5},{5,1},{2,6},{6,2},{3,7},{7,3},{8,12},{12,8},{9,1... | collective-permute-start | bytes 1966088 | tf_op jit(solution)/shard_map/ppermute | solution.py:279
  19.0 17.2 %collective-permute-start.12 = (bf16[80,1280]{1,0:T(8,128)(2,1)S(1)}, bf16[80,1280]{1,0:T(8,128)(2,1)S(1)}, u32[]{:S(2)}, u32[]{:S(2)}) collective-permute-start(bf16[80,1280]{1,0:T(8,128)(2,1)S(1)} %bitcast.38), channel_id=1, source_target_pairs={{0,16},{4,23},{16,1},{20,4},{1,17},{5,20},{17,2},{21,5},{2,18},{6,... | collective-permute-start | bytes 614408 | tf_op jit(solution)/shard_map/ppermute | solution.py:39
  25.4 17.9 %collective-permute-start.4 = (bf16[160,896]{1,0:T(8,128)(2,1)S(1)}, bf16[160,896]{1,0:T(8,128)(2,1)S(1)}, u32[]{:S(2)}, u32[]{:S(2)}) collective-permute-start(bf16[160,896]{1,0:T(8,128)(2,1)S(1)} %bitcast.35), channel_id=1, source_target_pairs={{0,19},{4,20},{16,0},{20,5},{1,16},{5,21},{17,1},{21,6},{2,17},{6,... | collective-permute-start | bytes 860168 | tf_op jit(solution)/shard_map/ppermute | solution.py:39
  27.3 19.9 %collective-permute-start.3 = (bf16[160,896]{1,0:T(8,128)(2,1)S(1)}, bf16[160,896]{1,0:T(8,128)(2,1)S(1)}, u32[]{:S(2)}, u32[]{:S(2)}) collective-permute-start(bf16[160,896]{1,0:T(8,128)(2,1)S(1)} %bitcast.36), channel_id=1, source_target_pairs={{0,16},{4,23},{16,1},{20,4},{1,17},{5,20},{17,2},{21,5},{2,18},{6,... | collective-permute-start | bytes 860168 | tf_op jit(solution)/shard_map/ppermute | solution.py:39
  33.4 20.0 %collective-permute-start.13 = (bf16[80,1280]{1,0:T(8,128)(2,1)S(1)}, bf16[80,1280]{1,0:T(8,128)(2,1)S(1)}, u32[]{:S(2)}, u32[]{:S(2)}) collective-permute-start(bf16[80,1280]{1,0:T(8,128)(2,1)S(1)} %bitcast.39), channel_id=1, source_target_pairs={{0,19},{4,20},{16,0},{20,5},{1,16},{5,21},{17,1},{21,6},{2,17},{6,... | collective-permute-start | bytes 614408 | tf_op jit(solution)/shard_map/ppermute | solution.py:39
  36.2 42.2 %copy-start.5 = (bf16[80,1280]{1,0:T(8,128)(2,1)}, bf16[80,1280]{1,0:T(8,128)(2,1)S(1)}, u32[]{:S(2)}) copy-start(bf16[80,1280]{1,0:T(8,128)(2,1)S(1)} %collective-permute-done.12.rest_1_) | copy-start | bytes 614404
  36.2 21.7 %collective-permute-start.14 = (bf16[80,1280]{1,0:T(8,128)(2,1)S(1)}, bf16[80,1280]{1,0:T(8,128)(2,1)S(1)}, u32[]{:S(2)}, u32[]{:S(2)}) collective-permute-start(bf16[80,1280]{1,0:T(8,128)(2,1)S(1)} %collective-permute-done.12.rest_1_), channel_id=1, source_target_pairs={{0,16},{4,23},{16,1},{20,4},{1,17},{5,20},{17,2},{21,5},{2,18},{6,... | collective-permute-start | bytes 614408 | tf_op jit(solution)/shard_map/ppermute | solution.py:39
  43.3 35.1 %collective-permute-start.6 = (bf16[160,896]{1,0:T(8,128)(2,1)S(1)}, bf16[160,896]{1,0:T(8,128)(2,1)S(1)}, u32[]{:S(2)}, u32[]{:S(2)}) collective-permute-start(bf16[160,896]{1,0:T(8,128)(2,1)S(1)} %collective-permute-done.4.rest_2_), channel_id=1, source_target_pairs={{0,19},{4,20},{16,0},{20,5},{1,16},{5,21},{17,1},{21,6},{2,17},{6,... | collective-permute-start | bytes 860168 | tf_op jit(solution)/shard_map/ppermute | solution.py:39
  47.2 37.9 %collective-permute-start.5 = (bf16[160,896]{1,0:T(8,128)(2,1)S(1)}, bf16[160,896]{1,0:T(8,128)(2,1)S(1)}, u32[]{:S(2)}, u32[]{:S(2)}) collective-permute-start(bf16[160,896]{1,0:T(8,128)(2,1)S(1)} %collective-permute-done.3.rest_1_), channel_id=1, source_target_pairs={{0,16},{4,23},{16,1},{20,4},{1,17},{5,20},{17,2},{21,5},{2,18},{6,... | collective-permute-start | bytes 860168 | tf_op jit(solution)/shard_map/ppermute | solution.py:39
  53.3 20.3 %collective-permute-start.15 = (bf16[80,1280]{1,0:T(8,128)(2,1)S(1)}, bf16[80,1280]{1,0:T(8,128)(2,1)}, u32[]{:S(2)}, u32[]{:S(2)}) collective-permute-start(bf16[80,1280]{1,0:T(8,128)(2,1)S(1)} %collective-permute-done.13.rest_2_), channel_id=1, source_target_pairs={{0,19},{4,20},{16,0},{20,5},{1,16},{5,21},{17,1},{21,6},{2,17},{6,... | collective-permute-start | bytes 614408 | tf_op jit(solution)/shard_map/ppermute | solution.py:39
  57.9 30.4 %copy-start.9 = (bf16[80,1280]{1,0:T(8,128)(2,1)}, bf16[80,1280]{1,0:T(8,128)(2,1)S(1)}, u32[]{:S(2)}) copy-start(bf16[80,1280]{1,0:T(8,128)(2,1)S(1)} %collective-permute-done.14.rest_3_) | copy-start | bytes 614404
  57.9 19.8 %collective-permute-start.16 = (bf16[80,1280]{1,0:T(8,128)(2,1)S(1)}, bf16[80,1280]{1,0:T(8,128)(2,1)S(1)}, u32[]{:S(2)}, u32[]{:S(2)}) collective-permute-start(bf16[80,1280]{1,0:T(8,128)(2,1)S(1)} %collective-permute-done.14.rest_3_), channel_id=1, source_target_pairs={{0,16},{4,23},{16,1},{20,4},{1,17},{5,20},{17,2},{21,5},{2,18},{6,... | collective-permute-start | bytes 614408 | tf_op jit(solution)/shard_map/ppermute | solution.py:39
  73.6 39.7 %collective-permute-start.17 = (bf16[80,1280]{1,0:T(8,128)(2,1)}, bf16[80,1280]{1,0:T(8,128)(2,1)S(1)}, u32[]{:S(2)}, u32[]{:S(2)}) collective-permute-start(bf16[80,1280]{1,0:T(8,128)(2,1)} %collective-permute-done.15.rest_4_), channel_id=1, source_target_pairs={{0,19},{4,20},{16,0},{20,5},{1,16},{5,21},{17,1},{21,6},{2,17},{6,... | collective-permute-start | bytes 614408 | tf_op jit(solution)/shard_map/ppermute | solution.py:39
  78.4 14.0 %collective-permute-start.8 = (bf16[160,896]{1,0:T(8,128)(2,1)S(1)}, bf16[160,896]{1,0:T(8,128)(2,1)S(1)}, u32[]{:S(2)}, u32[]{:S(2)}) collective-permute-start(bf16[160,896]{1,0:T(8,128)(2,1)S(1)} %collective-permute-done.6.rest_4_), channel_id=1, source_target_pairs={{0,19},{4,20},{16,0},{20,5},{1,16},{5,21},{17,1},{21,6},{2,17},{6,... | collective-permute-start | bytes 860168 | tf_op jit(solution)/shard_map/ppermute | solution.py:39
  85.2 17.9 %collective-permute-start.7 = (bf16[160,896]{1,0:T(8,128)(2,1)S(1)}, bf16[160,896]{1,0:T(8,128)(2,1)S(1)}, u32[]{:S(2)}, u32[]{:S(2)}) collective-permute-start(bf16[160,896]{1,0:T(8,128)(2,1)S(1)} %collective-permute-done.5.rest_3_), channel_id=1, source_target_pairs={{0,16},{4,23},{16,1},{20,4},{1,17},{5,20},{17,2},{21,5},{2,18},{6,... | collective-permute-start | bytes 860168 | tf_op jit(solution)/shard_map/ppermute | solution.py:39
  93.1 29.9 %collective-permute-start.10 = (bf16[80,896]{1,0:T(8,128)(2,1)}, bf16[80,896]{1,0:T(8,128)(2,1)}, u32[]{:S(2)}, u32[]{:S(2)}) collective-permute-start(bf16[80,896]{1,0:T(8,128)(2,1)} %slice.32), channel_id=1, source_target_pairs={{0,19},{4,20},{16,0},{20,5},{1,16},{5,21},{17,1},{21,6},{2,17},{6,... | collective-permute-start | bytes 430088 | tf_op jit(solution)/shard_map/ppermute | solution.py:39
  103.7 19.3 %collective-permute-start.9 = (bf16[80,896]{1,0:T(8,128)(2,1)}, bf16[80,896]{1,0:T(8,128)(2,1)}, u32[]{:S(2)}, u32[]{:S(2)}) collective-permute-start(bf16[80,896]{1,0:T(8,128)(2,1)} %slice.31), channel_id=1, source_target_pairs={{0,16},{4,23},{16,1},{20,4},{1,17},{5,20},{17,2},{21,5},{2,18},{6,... | collective-permute-start | bytes 430088 | tf_op jit(solution)/shard_map/ppermute | solution.py:39
  106.5 16.5 %collective-permute-start.2 = (bf16[8,1280]{1,0:T(8,128)(2,1)}, bf16[8,1280]{1,0:T(8,128)(2,1)}, u32[]{:S(2)}, u32[]{:S(2)}) collective-permute-start(bf16[8,1280]{1,0:T(8,128)(2,1)} %slice.28), channel_id=1, source_target_pairs={{0,16},{1,17},{2,18},{3,19},{4,20},{5,21},{6,22},{7,23},{8,24},{9,... | collective-permute-start | bytes 61448 | tf_op jit(solution)/shard_map/ppermute | solution.py:329
  107.8 25.8 %collective-permute-start.18 = (bf16[80,640]{1,0:T(8,128)(2,1)}, bf16[80,640]{1,0:T(8,128)(2,1)S(1)}, u32[]{:S(2)}, u32[]{:S(2)}) collective-permute-start(bf16[80,640]{1,0:T(8,128)(2,1)} %slice.33), channel_id=1, source_target_pairs={{0,16},{4,23},{16,1},{20,4},{1,17},{5,20},{17,2},{21,5},{2,18},{6,... | collective-permute-start | bytes 307208 | tf_op jit(solution)/shard_map/ppermute | solution.py:39
  114.0 19.6 %collective-permute-start.19 = (bf16[80,640]{1,0:T(8,128)(2,1)}, bf16[80,640]{1,0:T(8,128)(2,1)}, u32[]{:S(2)}, u32[]{:S(2)}) collective-permute-start(bf16[80,640]{1,0:T(8,128)(2,1)} %slice.34), channel_id=1, source_target_pairs={{0,19},{4,20},{16,0},{20,5},{1,16},{5,21},{17,1},{21,6},{2,17},{6,... | collective-permute-start | bytes 307208 | tf_op jit(solution)/shard_map/ppermute | solution.py:39
  124.0 16.0 %copy-start.8 = (bf16[80,1280]{1,0:T(8,128)(2,1)S(1)}, bf16[80,1280]{1,0:T(8,128)(2,1)}, u32[]{:S(2)}) copy-start(bf16[80,1280]{1,0:T(8,128)(2,1)} %copy-done.7) | copy-start | bytes 614404
  124.0 16.0 %copy-start.10 = (bf16[80,1280]{1,0:T(8,128)(2,1)S(1)}, bf16[80,1280]{1,0:T(8,128)(2,1)}, u32[]{:S(2)}) copy-start(bf16[80,1280]{1,0:T(8,128)(2,1)} %copy-done.9) | copy-start | bytes 614404
  132.1 7.8 %collective-permute-start.11 = (bf16[64,640]{1,0:T(8,128)(2,1)S(1)}, bf16[64,640]{1,0:T(8,128)(2,1)S(1)}, u32[]{:S(2)}, u32[]{:S(2)}) collective-permute-start(bf16[64,640]{1,0:T(8,128)(2,1)S(1)} %get-tuple-element.22), channel_id=1, source_target_pairs={{0,16},{1,17},{2,18},{3,19},{4,20},{5,21},{6,22},{7,23},{8,24},{9,... | collective-permute-start | bytes 245768 | tf_op jit(solution)/shard_map/ppermute | solution.py:359
  142.8 16.1 %copy-start = (bf16[1,1,128,1280]{3,2,1,0:T(8,128)(2,1)S(1)}, bf16[1,1,128,1280]{3,2,1,0:T(8,128)(2,1)}, u32[]{:S(2)}) copy-start(bf16[1,1,128,1280]{3,2,1,0:T(8,128)(2,1)} %rows.3) | copy-start | bytes 983044
  142.8 4.5 %collective-permute-start.20 = (bf16[2,128,768]{2,1,0:T(8,128)(2,1)S(1)}, bf16[2,128,768]{2,1,0:T(8,128)(2,1)S(1)}, u32[]{:S(2)}, u32[]{:S(2)}) collective-permute-start(bf16[2,128,768]{2,1,0:T(8,128)(2,1)S(1)} %get-tuple-element.24), channel_id=1, source_target_pairs={{0,4},{4,0},{1,5},{5,1},{2,6},{6,2},{3,7},{7,3},{8,12},{12,8},{9,1... | collective-permute-start | bytes 1179656 | tf_op jit(solution)/shard_map/ppermute | solution.py:279
  144.9 8.3 %collective-permute-start.23 = (bf16[2,128,640]{2,1,0:T(8,128)(2,1)S(1)}, bf16[2,128,640]{2,1,0:T(8,128)(2,1)S(1)}, u32[]{:S(2)}, u32[]{:S(2)}) collective-permute-start(bf16[2,128,640]{2,1,0:T(8,128)(2,1)S(1)} %get-tuple-element.29), channel_id=1, source_target_pairs={{0,4},{4,0},{1,5},{5,1},{2,6},{6,2},{3,7},{7,3},{8,12},{12,8},{9,1... | collective-permute-start | bytes 983048 | tf_op jit(solution)/shard_map/ppermute | solution.py:279
  147.5 11.4 %collective-permute-start.21 = (bf16[128,768]{1,0:T(8,128)(2,1)S(1)}, bf16[128,768]{1,0:T(8,128)(2,1)S(1)}, u32[]{:S(2)}, u32[]{:S(2)}) collective-permute-start(bf16[128,768]{1,0:T(8,128)(2,1)S(1)} %get-tuple-element.26), channel_id=1, source_target_pairs={{0,8},{8,0},{1,9},{9,1},{2,10},{10,2},{3,11},{11,3},{4,12},{12,4},... | collective-permute-start | bytes 589832 | tf_op jit(solution)/shard_map/ppermute | solution.py:279
  153.2 8.5 %collective-permute-start.24 = (bf16[128,640]{1,0:T(8,128)(2,1)S(1)}, bf16[128,640]{1,0:T(8,128)(2,1)S(1)}, u32[]{:S(2)}, u32[]{:S(2)}) collective-permute-start(bf16[128,640]{1,0:T(8,128)(2,1)S(1)} %get-tuple-element.31), channel_id=1, source_target_pairs={{0,8},{8,0},{1,9},{9,1},{2,10},{10,2},{3,11},{11,3},{4,12},{12,4},... | collective-permute-start | bytes 491528 | tf_op jit(solution)/shard_map/ppermute | solution.py:279
  161.8 11.3 %collective-permute-start.25 = (bf16[128,640]{1,0:T(8,128)(2,1)S(1)}, bf16[128,640]{1,0:T(8,128)(2,1)S(1)}, u32[]{:S(2)}, u32[]{:S(2)}) collective-permute-start(bf16[128,640]{1,0:T(8,128)(2,1)S(1)} %shard_map.115), channel_id=1, source_target_pairs={{0,32},{32,64},{64,96},{96,128},{128,160},{160,192},{192,224},{224... | collective-permute-start | bytes 491528 | tf_op jit(solution)/shard_map/ppermute | solution.py:408
  165.2 11.0 %collective-permute-start.22 = (bf16[128,640]{1,0:T(8,128)(2,1)S(1)}, bf16[128,640]{1,0:T(8,128)(2,1)S(1)}, u32[]{:S(2)}, u32[]{:S(2)}) collective-permute-start(bf16[128,640]{1,0:T(8,128)(2,1)S(1)} %get-tuple-element.27), channel_id=1, source_target_pairs={{0,32},{32,64},{64,96},{96,128},{128,160},{160,192},{192,224},{224... | collective-permute-start | bytes 491528 | tf_op jit(solution)/shard_map/ppermute | solution.py:407
  (15 other events, 69.6 us)
